TPU v7x, 32 devices: a whole 2x2x4 slice. The times are simulated.
32 devices in a mesh: rep: 4 (over y, x), dom: 8 (over z, core).
Axes of the slice: x: 2, y: 2, z: 4, core: 2. Of those that a mesh axis runs over, the one named last changes fastest.
Arguments:
- node_pos: float32 [3, 16384], P(None, 'dom'), may hold values from -6 to 6
- node_order: int32 [8, 2048], P('dom'), may hold values from 0 to 2047, each once within a row
- facet_centroid: float32 [3, 16384], P(None, 'dom'), may hold values from -6 to 6
- facet_normal: float32 [3, 16384], P(None, 'dom'), may hold values from -6 to 6
- facet_nodes: int32 [3, 16384], P(None, 'dom'), may hold values from 0 to 2047
- pair_bucket: int32 [4, 8, 128], P('rep', 'dom'), may hold values from 0 to 15
- pair_owner: int32 [4, 8, 128, 1], P('rep', 'dom'), may hold values from 0 to 7; in each aligned block of 128 rows (0 to 127, 128 to 255, ..., all dimensions but the last counted through in order) at most 32 rows name the same one
- pair_slot: int32 [4, 8, 128], P('rep', 'dom'), may hold values from 0 to 15
- pair_count: int32 [4, 8], P('rep', 'dom'), may hold values from 64 to 128, as said below
Outputs:
- node_force: float32 [3, 16384], P(None, 'dom')
Inputs may be any that keep to these rules, and one draw needn't show every extreme that they name: `pair_owner`: among the 128 pairs of one device, each domain is named at most 32 times, and exactly 32 times in some device's pairs. `pair_count`: some device uses all 128 pairs. `node_order`: each row is a permutation.
All inputs are finite; a program needn't handle non-finite values.
Results may differ from a plain program's by a relative error of at most 0.00013.
Values sent between devices are 32-bit elements; how exact they have to be, the bound alone decides.
A program may use at most 64 MiB of HBM per device.

v0:
```python
import jax
import jax.numpy as jnp
from jax import lax
from jax.sharding import PartitionSpec as P

BUCKET = 128
PAIRS_DEV = 128


STIFFNESS = 0.125
RADIUS_SQ = 4.0
pair_block = 8


def tile_terms(facet_geom, node_points):
    centre = facet_geom[:, 0:3]
    normal = facet_geom[:, 3:6]
    delta = node_points[:, :, None, :] - centre[:, :, :, None]
    gap = jnp.sum(normal[:, :, :, None] * delta, axis=1)
    dist = jnp.sum(delta * delta, axis=1)
    strength = STIFFNESS * jax.nn.softplus(-gap) * jnp.exp(-dist / RADIUS_SQ)
    node_term = jnp.einsum("bkf,bfp->bkp", normal, strength, precision=lax.Precision.HIGHEST)
    reaction = -normal * jnp.sum(strength, axis=2)[:, None, :]
    return (node_term, reaction)


def slot_numbers(owners, is_live, per_owner, dummy_slot):
    rows = owners.shape[0]
    positions = jnp.arange(rows, dtype=jnp.int32)
    earlier = (
        (positions[None, :] < positions[:, None])
        & (owners[None, :] == owners[:, None])
        & is_live[None, :]
    )
    ranking = jnp.sum(earlier.astype(jnp.int32), axis=1)
    return jnp.where(is_live, owners * per_owner + ranking, dummy_slot)


def pair_loop(
    live_count, geom_rows, point_rows, slot_index, bucket_index, is_live, slot_total, bucket_total
):
    width = geom_rows.shape[2]
    geom_pad = jnp.concatenate([geom_rows, jnp.zeros((pair_block, 6, width), jnp.float32)], 0)
    point_pad = jnp.concatenate([point_rows, jnp.zeros((pair_block, 3, width), jnp.float32)], 0)
    slot_pad = jnp.concatenate([slot_index, jnp.full((pair_block,), slot_total, jnp.int32)])
    bucket_pad = jnp.concatenate([bucket_index, jnp.zeros((pair_block,), jnp.int32)])
    live_pad = jnp.concatenate([is_live, jnp.zeros((pair_block,), jnp.bool_)])

    def step(block_index, carry):
        slot_acc, bucket_acc = carry
        start = block_index * pair_block
        facet_geom = lax.dynamic_slice_in_dim(geom_pad, start, pair_block)
        node_points = lax.dynamic_slice_in_dim(point_pad, start, pair_block)
        slot_take = lax.dynamic_slice_in_dim(slot_pad, start, pair_block)
        bucket_take = lax.dynamic_slice_in_dim(bucket_pad, start, pair_block)
        weight = lax.dynamic_slice_in_dim(live_pad, start, pair_block).astype(jnp.float32)
        node_term, reaction = tile_terms(facet_geom, node_points)
        slot_acc = slot_acc.at[slot_take].add(node_term * weight[:, None, None])
        bucket_acc = bucket_acc.at[bucket_take].add(reaction * weight[:, None, None])
        return (slot_acc, bucket_acc)

    blocks = (live_count + pair_block - 1) // pair_block
    start_acc = (
        jnp.zeros((slot_total + 1, 3, width), jnp.float32),
        jnp.zeros((bucket_total, 3, width), jnp.float32),
    )
    return lax.fori_loop(jnp.int32(0), blocks, step, start_acc)


def per_device(
    node_pos,
    node_order,
    facet_centroid,
    facet_normal,
    facet_nodes,
    pair_bucket,
    pair_owner,
    pair_slot,
    pair_count,
):
    domains = lax.axis_size("dom")
    per_owner = max(2, 2 * PAIRS_DEV // domains)
    slot_total = domains * per_owner
    width = BUCKET
    node_buckets = node_pos.shape[1] // width
    facet_buckets = facet_centroid.shape[1] // width
    bucket_points = node_pos[:, node_order[0]].reshape(3, node_buckets, width).transpose(1, 0, 2)
    bucket_geom = (
        jnp.concatenate([facet_centroid, facet_normal], 0)
        .reshape(6, facet_buckets, width)
        .transpose(1, 0, 2)
    )
    owners = pair_owner[0, 0, :, 0]
    buckets = pair_bucket[0, 0]
    slots = pair_slot[0, 0]
    rows = buckets.shape[0]
    positions = jnp.arange(rows, dtype=jnp.int32)
    is_live = positions < pair_count[0, 0]
    live_count = jnp.sum(is_live.astype(jnp.int32))
    slot_index = slot_numbers(owners, is_live, per_owner, slot_total)
    request = (
        jnp.full((slot_total + 1,), -1, jnp.int32)
        .at[slot_index]
        .set(slots)[:-1]
        .reshape(domains, per_owner)
    )
    every_bucket = lax.all_gather(bucket_points, "dom", axis=0, tiled=True)
    point_rows = every_bucket[owners * node_buckets + slots]
    slot_acc, facet_acc = pair_loop(
        live_count,
        bucket_geom[buckets],
        point_rows,
        slot_index,
        buckets,
        is_live,
        slot_total,
        facet_buckets,
    )
    home_blocks, home_slots = (
        lax.all_to_all(
            slot_acc[:-1].reshape(domains, per_owner, 3, width),
            "dom",
            split_axis=0,
            concat_axis=0,
            tiled=True,
        ),
        lax.all_to_all(request.astype(jnp.float32), "dom", split_axis=0, concat_axis=0, tiled=True),
    )
    home_slots = home_slots.reshape(slot_total).astype(jnp.int32)
    home_blocks = home_blocks.reshape(slot_total, 3, width)
    target = jnp.where(home_slots >= 0, home_slots, node_buckets)
    bucket_force = (
        jnp.zeros((node_buckets + 1, 3, width), jnp.float32).at[target].add(home_blocks)[:-1]
    )
    node_force = (
        jnp.zeros((3, node_pos.shape[1]), jnp.float32)
        .at[:, node_order[0]]
        .add(bucket_force.transpose(1, 0, 2).reshape(3, -1))
    )
    reaction = facet_acc.transpose(1, 0, 2).reshape(3, -1) / 3.0
    for corner in range(3):
        node_force = node_force.at[:, facet_nodes[corner]].add(reaction)
    return lax.psum(node_force, "rep")


def solution(mesh):
    placed = (
        P(None, "dom"),
        P("dom", None),
        P(None, "dom"),
        P(None, "dom"),
        P(None, "dom"),
        P("rep", "dom", None),
        P("rep", "dom", None, None),
        P("rep", "dom", None),
        P("rep", "dom"),
    )
    return jax.shard_map(
        per_device, mesh=mesh, in_specs=placed, out_specs=P(None, "dom"), check_vma=False
    )
```

profile of v0, /device:TPU:0, one launch (start us, length us, event | category | flops | bytes accessed | tf_op | source)
XLA Modules:
  0.0 215.2 jit_solution(11657129899521065713)
XLA Ops:
  0.7 0.9 convert_reduce_fusion
  1.6 0.7 fusion.11
  2.3 1.1 scatter_custom_fusion.2
  3.4 0.7 convert_element_type.37
  4.1 6.4 %all-to-all-start = ((f32[8,1,32]{2,1,0:T(1,128)}), f32[8,1,32]{2,1,0:T(1,128)S(1)}, u32[]{:S(2)}, u32[]{:S(2)}) async-start(f32[8,1,32]{2,1,0:T(1,128)} %convert_element_type.37), calls=%async_computation | async-start | bytes 8192 | tf_op jit(solution)/shard_map/all_to_all | solution.py:127
  10.4 0.6 convert_reduce_fusion.2
  11.6 0.7 compare_select_fusion.6
  12.4 1.1 copy.46
  13.5 5.5 %gather_fusion.1 = f32[2048,3]{1,0:T(8,128)S(1)} fusion(f32[3,2048]{0,1:T(8,128)S(1)} %copy.46, s32[2048]{0:T(1024)S(1)} %broadcast_clamp_fusion), kind=kCustom, calls=%fused_computation.1 | custom fusion | bytes 57344 | tf_op jit(solution)/shard_map/gather | solution.py:87
  19.3 14.8 %all_gather.3 = f32[128,3,128]{2,0,1:T(8,128)S(1)} all-gather(f32[16,3,128]{2,0,1:T(8,128)S(1)} %bitcast.77), channel_id=1, replica_groups=mesh['rep'=4,'dom'=8] {'dom'}, dimensions={0}, use_global_device_ids=true | all-gather | bytes 221184 | tf_op jit(solution)/shard_map/all_gather | solution.py:107
  34.3 0.8 gather_fusion.2
  35.1 0.8 gather_fusion
  36.1 31.3 %while.12 = (s32[]{:T(128)}, f32[257,3,128]{2,1,0:T(4,128)S(1)}, f32[16,3,128]{2,1,0:T(4,128)S(1)}, s32[]{:T(128)}, s32[136]{0:T(256)S(1)}, /*index=5*/f32[136,6...) while((s32[]{:T(128)}, f32[257,3,128]{2,1,0:T(4,128)S(1)}, ...), condition=%wide.region_9.10_spmd, body=%wide.region_3.9_spmd.sunk | while | flops 8012863 | bytes 3387895 | solution.py:67
  36.1 1.0 fusion.23
  37.7 0.5 convolution_multiply_fusion.2
  38.3 0.8 scatter_fusion
  39.2 0.8 scatter_fusion.1
  40.1 1.0 fusion.23
  42.3 0.8 scatter_fusion
  43.1 0.8 scatter_fusion.1
  44.0 1.0 fusion.23
  46.2 0.8 scatter_fusion
  47.0 0.8 scatter_fusion.1
  47.9 1.0 fusion.23
  50.1 0.8 scatter_fusion
  50.9 0.8 scatter_fusion.1
  51.8 1.0 fusion.23
  54.0 0.8 scatter_fusion
  54.8 0.8 scatter_fusion.1
  55.7 1.0 fusion.23
  57.9 0.8 scatter_fusion
  58.8 0.8 scatter_fusion.1
  59.6 1.0 fusion.23
  61.8 0.8 scatter_fusion
  62.7 0.8 scatter_fusion.1
  63.5 1.0 fusion.23
  65.7 0.8 scatter_fusion
  66.6 0.8 scatter_fusion.1
  67.5 0.8 copy.50
  68.6 35.8 %all-to-all-start.1 = ((f32[8,32,3,128]{3,1,2,0:T(8,128)}), f32[8,32,3,128]{3,1,2,0:T(8,128)S(1)}, u32[]{:S(2)}, u32[]{:S(2)}) async-start(f32[8,32,3,128]{3,1,2,0:T(8,128)} %copy.50), calls=%async_computation.1 | async-start | bytes 786432 | tf_op jit(solution)/shard_map/all_to_all | solution.py:120
  104.6 12.4 %all-to-all-done.1 = f32[8,32,3,128]{3,1,2,0:T(8,128)S(1)} async-done(((f32[8,32,3,128]{3,1,2,0:T(8,128)}), f32[8,32,3,128]{3,1,2,0:T(8,128)S(1)}, u32[]{:S(2)}, u32[]{:S(2)}) %all-to-all-start.1) | async-done | bytes 393248 | tf_op jit(solution)/shard_map/all_to_all | solution.py:120
  117.3 8.8 %scatter_fusion.2 = f32[17,3,128]{2,1,0:T(4,128)S(1)} fusion(f32[17,3,128]{2,1,0:T(4,128)S(1)} %broadcast_in_dim.32, s32[256]{0:T(256)S(1)} %bitcast.84, f32[256,3,128]{2,1,0:T(4,128)S(1)} %copy.52), kind=kCustom, calls=%fused_computation.6 | custom fusion | flops 98304 | bytes 1180672 | tf_op jit(solution)/shard_map/scatter-add | solution.py:133
  126.5 11.7 %scatter_custom_fusion.4 = f32[3,2048]{0,1:T(8,128)S(1)} fusion(s32[2048]{0:T(1024)S(1)} %bitcast.82, f32[2048,3]{1,0:T(8,128)S(1)} %copy.53, f32[]{:T(128)} %constant.33.clone.1), kind=kCustom, calls=%fused_computation.26 | custom fusion | flops 6144 | bytes 24580 | tf_op jit(solution)/shard_map/scatter-add | solution.py:138
  138.2 11.9 %scatter_fusion.3 = f32[3,2048]{0,1:T(8,128)S(1)} fusion(f32[3,2048]{0,1:T(8,128)S(1)} %scatter_custom_fusion.4, s32[2048]{0:T(1024)S(1)} %bitcast.80, f32[2048,3]{1,0:T(8,128)S(1)} %copy.54), kind=kCustom, calls=%fused_computation.8 | custom fusion | flops 6144 | bytes 81920 | tf_op jit(solution)/shard_map/scatter-add | solution.py:142
  150.1 12.1 %scatter_fusion.4 = f32[3,2048]{0,1:T(8,128)S(1)} fusion(f32[3,2048]{0,1:T(8,128)S(1)} %scatter_fusion.3, s32[2048]{0:T(1024)S(1)} %bitcast.79, f32[2048,3]{1,0:T(8,128)S(1)} %copy.54), kind=kCustom, calls=%fused_computation.9 | custom fusion | flops 6144 | bytes 81920 | tf_op jit(solution)/shard_map/scatter-add | solution.py:142
  162.1 11.9 %scatter_fusion.5 = f32[3,2048]{0,1:T(8,128)S(1)} fusion(f32[3,2048]{0,1:T(8,128)S(1)} %scatter_fusion.4, s32[2048]{0:T(1024)S(1)} %bitcast.78, f32[2048,3]{1,0:T(8,128)S(1)} %copy.54), kind=kCustom, calls=%fused_computation.10 | custom fusion | flops 6144 | bytes 81920 | tf_op jit(solution)/shard_map/scatter-add | solution.py:142
  174.0 40.3 %psum.7 = f32[3,2048]{0,1:T(8,128)S(1)} all-reduce(f32[3,2048]{0,1:T(8,128)S(1)} %scatter_fusion.5), channel_id=1, replica_groups=mesh['rep'=4,'dom'=8] {'rep'}, use_global_device_ids=true, to_apply=%region_15.16 | all-reduce | flops 6144 | bytes 49152 | tf_op jit(solution)/shard_map/psum | solution.py:143
  214.3 0.9 copy.57
  (88 shorter events, 11.4 us)
Async XLA Ops:
  4.1 64.5 %all-to-all-start = ((f32[8,1,32]{2,1,0:T(1,128)}), f32[8,1,32]{2,1,0:T(1,128)S(1)}, u32[]{:S(2)}, u32[]{:S(2)}) async-start(f32[8,1,32]{2,1,0:T(1,128)} %convert_element_type.37), calls=%async_computation | async-start | bytes 8192 | tf_op jit(solution)/shard_map/all_to_all | solution.py:127
  13.5 20.7 %copy-start.3 = (s32[1,1,128,1]{2,3,1,0:T(1,128)S(1)}, s32[1,1,128,1]{2,3,1,0:T(1,128)}, u32[]{:S(2)}) copy-start(s32[1,1,128,1]{2,3,1,0:T(1,128)} %param.17) | copy-start | bytes 1540
  13.5 20.8 %copy-start.4 = (s32[1,1,128]{2,1,0:T(1,128)S(1)}, s32[1,1,128]{2,1,0:T(1,128)}, u32[]{:S(2)}) copy-start(s32[1,1,128]{2,1,0:T(1,128)} %param.16) | copy-start | bytes 1540
  19.3 15.8 %copy-start = (f32[3,2048]{1,0:T(4,128)S(1)}, f32[3,2048]{1,0:T(4,128)}, u32[]{:S(2)}) copy-start(f32[3,2048]{1,0:T(4,128)} %param.14) | copy-start | bytes 73732
  19.3 15.8 %copy-start.1 = (f32[3,2048]{1,0:T(4,128)S(1)}, f32[3,2048]{1,0:T(4,128)}, u32[]{:S(2)}) copy-start(f32[3,2048]{1,0:T(4,128)} %param.13) | copy-start | bytes 73732
  68.2 36.2 %copy-start.2 = (s32[3,2048]{1,0:T(4,128)S(1)}, s32[3,2048]{1,0:T(4,128)}, u32[]{:S(2)}) copy-start(s32[3,2048]{1,0:T(4,128)} %param.15) | copy-start | bytes 73732
  68.6 48.4 %all-to-all-start.1 = ((f32[8,32,3,128]{3,1,2,0:T(8,128)}), f32[8,32,3,128]{3,1,2,0:T(8,128)S(1)}, u32[]{:S(2)}, u32[]{:S(2)}) async-start(f32[8,32,3,128]{3,1,2,0:T(8,128)} %copy.50), calls=%async_computation.1 | async-start | bytes 786432 | tf_op jit(solution)/shard_map/all_to_all | solution.py:120
where the time goes:
time: 216 us; the launch traced here: 215 us
  other arithmetic  85.8 us (40%)
  blocking collectives  55 us (25%)
  starting transfers between devices  42.2 us (20%)
  local copies, waits for them, and re-layouts  13.6 us (6%)
  waiting for transfers between devices  12.4 us (6%)
  matrix products  4.18 us (2%)
    psum x1, blocking collectives, per_device(): return lax.psum(node_force, 'rep')  40.3 us
    all_to_all x1, starting transfers between devices, per_device(): lax.all_to_all(slot_acc[:-1].reshape(domains, per_owner, 3, width), 'dom'...  35.8 us
    scatter-add x3, other arithmetic, per_device(): node_force = node_force.at[:, facet_nodes[corner]].add(reaction)  35.8 us
    all_gather x1, blocking collectives, per_device(): every_bucket = lax.all_gather(bucket_points, 'dom', axis=0, tiled=True)  14.8 us
    all_to_all x1, waiting for transfers between devices, per_device(): lax.all_to_all(slot_acc[:-1].reshape(domains, per_owner, 3, width), 'dom'...  12.4 us
    scatter-add x1, other arithmetic, per_device(): node_force = jnp.zeros((3, node_pos.shape[1]), jnp.float32).at[:, node_or...  11.7 us
    scatter-add x1, other arithmetic, per_device(): jnp.zeros((node_buckets + 1, 3, width), jnp.float32).at[target]  8.8 us
    reduce_sum x8, other arithmetic, tile_terms(): gap = jnp.sum(normal[:, :, :, None] * delta, axis=1)  8.29 us
  transfers between devices with their start and end apart: 2, of which 1 were waited for; matrix products, arithmetic and copies ran while one was open for 20% of the time, Pallas kernels for 0%

commit v1 on v0

v1 whole, which is shorter than its diff:
```python
import functools

import jax
import jax.numpy as jnp
from jax import lax
from jax.experimental import pallas as pl
from jax.experimental.pallas import tpu as pltpu
from jax.sharding import PartitionSpec as P

BUCKET = 128
STIFFNESS = 0.125
RADIUS_SQ = 4.0
LOG2E = 1.4426950408889634
MESH_ID = pl.DeviceIdType.MESH
VMEM = pl.BlockSpec(memory_space=pltpu.VMEM)
SMEM = pl.BlockSpec(memory_space=pltpu.SMEM)
F32 = jnp.float32
BF16 = jnp.bfloat16


def repeat(count, body):
    if count <= 16:
        for i in range(count):
            body(i)
    else:
        def step(i, carry):
            body(i)
            return carry

        lax.fori_loop(0, count, step, 0)


def split3(value):
    first = value.astype(BF16).astype(F32)
    rest = value - first
    second = rest.astype(BF16).astype(F32)
    return first, second, rest - second


def gather_kernel(domains, pos_ref, order_ref, out_ref, send_sem, recv_sem):
    me = lax.axis_index("dom")
    rows = out_ref.shape[0] // domains
    buckets = rows // 3
    barrier = pltpu.get_barrier_semaphore()

    def greet(t):
        peer = lax.rem(me + t + 1, domains)
        pl.semaphore_signal(barrier, inc=1, device_id={"dom": peer}, device_id_type=MESH_ID)

    repeat(domains - 1, greet)

    order = jnp.concatenate(
        [order_ref[:, h * BUCKET : (h + 1) * BUCKET] for h in range(buckets)], 0
    )
    high = lax.div(order, BUCKET)
    low = order - high * BUCKET
    own = pl.multiple_of(me * rows, 8)
    for k in range(3):
        picked = jnp.zeros((buckets, BUCKET), F32)
        for h in range(buckets):
            row = jnp.broadcast_to(
                pos_ref[k : k + 1, h * BUCKET : (h + 1) * BUCKET], (buckets, BUCKET)
            )
            found = jnp.take_along_axis(row, low, axis=1, mode="promise_in_bounds")
            picked = jnp.where(high == h, found, picked)
        out_ref[pl.ds(own + k * buckets, buckets), :] = picked

    pl.semaphore_wait(barrier, domains - 1)
    block = out_ref.at[pl.ds(own, rows)]

    def copy_to(t):
        peer = lax.rem(me + t + 1, domains)
        return pltpu.make_async_remote_copy(
            src_ref=block,
            dst_ref=block,
            send_sem=send_sem.at[t],
            recv_sem=recv_sem.at[t],
            device_id={"dom": peer},
            device_id_type=MESH_ID,
        )

    def copy_from(t):
        source = lax.rem(me + 2 * domains - t - 1, domains)
        landed = out_ref.at[pl.ds(pl.multiple_of(source * rows, 8), rows)]
        return pltpu.make_async_remote_copy(
            src_ref=landed,
            dst_ref=landed,
            send_sem=send_sem.at[t],
            recv_sem=recv_sem.at[t],
            device_id={"dom": source},
            device_id_type=MESH_ID,
        )

    repeat(domains - 1, lambda t: copy_to(t).start())
    repeat(domains - 1, lambda t: copy_from(t).wait_recv())
    repeat(domains - 1, lambda t: copy_to(t).wait_send())


def pair_kernel(
    node_buckets,
    count_ref,
    bucket_ref,
    owner_ref,
    slot_ref,
    points_ref,
    centre_ref,
    normal_ref,
    nodes_ref,
    rows_ref,
    geom_ref,
    wide_ref,
    sum_ref,
):
    facet_buckets = centre_ref.shape[1] // BUCKET
    nodes_ref[...] = jnp.zeros_like(nodes_ref)
    sum_ref[...] = jnp.zeros_like(sum_ref)
    scale = LOG2E / RADIUS_SQ
    nothing = jnp.zeros((1, BUCKET), F32)

    def prepare(b, carry):
        at = pl.ds(pl.multiple_of(b * BUCKET, BUCKET), BUCKET)
        n = [normal_ref[k : k + 1, at] for k in range(3)]
        c = [centre_ref[k : k + 1, at] for k in range(3)]
        n_c = n[0] * c[0] + n[1] * c[1] + n[2] * c[2]
        c_c = c[0] * c[0] + c[1] * c[1] + c[2] * c[2]
        gap = jnp.concatenate([-n[0], -n[1], -n[2], nothing, n_c] + [nothing] * 3, 0)
        dist = jnp.concatenate(
            [2.0 * scale * c[0], 2.0 * scale * c[1], 2.0 * scale * c[2]]
            + [nothing - scale, -scale * c_c] + [nothing] * 3,
            0,
        )
        raw = jnp.concatenate(n + [nothing] * 5, 0)
        blank = jnp.zeros((BUCKET - 56, BUCKET), F32)
        for part, rows in enumerate((gap, dist)):
            a, bb, cc = split3(rows)
            table = jnp.concatenate([a, bb, cc, a, bb, a, raw, blank], 0).T
            geom_ref[b, part * BUCKET : (part + 1) * BUCKET, :] = table.astype(BF16)
            if part == 0:
                for k in range(3):
                    wide_ref[b, k] = jnp.broadcast_to(table[:, 48 + k : 49 + k], (BUCKET, BUCKET))
        return carry

    lax.fori_loop(0, facet_buckets, prepare, 0)

    count = count_ref[0, 0]
    place = lax.broadcasted_iota(jnp.int32, (8, BUCKET), 0)
    blank = jnp.zeros((BUCKET - 48, BUCKET), F32)
    spare = nodes_ref.shape[0] - 3 * node_buckets

    def one(p):
        live = p < count
        b = bucket_ref[p]
        base = owner_ref[p] * (3 * node_buckets) + slot_ref[p]
        x, y, z = (
            jnp.broadcast_to(points_ref[pl.ds(base + k * node_buckets, 1), :], (8, BUCKET))
            for k in range(3)
        )
        square = x * x + y * y + z * z
        one_or_zero = jnp.where(place == 4, 1.0, 0.0)
        value = jnp.where(place == 3, square, one_or_zero)
        value = jnp.where(place == 2, z, value)
        value = jnp.where(place == 1, y, value)
        value = jnp.where(place == 0, x, value)
        v1, v2, v3 = split3(value)
        table = jnp.concatenate([v1, v1, v1, v2, v2, v3, blank], 0).astype(BF16)
        both = jnp.dot(geom_ref[b], table, preferred_element_type=F32)
        minus_gap, fade = both[:BUCKET], both[BUCKET:]
        small = jnp.exp(-jnp.abs(minus_gap))
        logs = jnp.where(small < 2.0**-8, small * (1.0 - 0.5 * small), jnp.log(1.0 + small))
        strength = (jnp.maximum(minus_gap, 0.0) + logs) * jnp.exp2(fade)
        to_bucket = jnp.where(live, b, facet_buckets)
        to_node = jnp.where(live, base, spare)
        sum_ref[to_bucket] += strength
        for k in range(3):
            term = jnp.sum(wide_ref[b, k] * strength, axis=0, keepdims=True)
            nodes_ref[pl.ds(to_node + k * node_buckets, 1), :] += term

    def step(i, carry):
        one(2 * i)
        one(2 * i + 1)
        return carry

    lax.fori_loop(0, lax.div(count + 1, 2), step, 0)

    for b in range(facet_buckets):
        rows_ref[b : b + 1, :] = jnp.sum(sum_ref[b].T, axis=0, keepdims=True)


def exchange_kernel(
    domains,
    copies,
    nodes_ref,
    rows_ref,
    nodes_out,
    rows_out,
    landed,
    landed_rows,
    total,
    landed_total,
    send_sem,
    recv_sem,
    send_row,
    recv_row,
    send_total,
    recv_total,
):
    me = lax.axis_index("dom")
    rep = lax.axis_index("rep")
    size = landed.shape[1]
    barrier = pltpu.get_barrier_semaphore()

    def dom_peer(t):
        return lax.rem(me + t + 1, domains)

    def rep_peer(t):
        return lax.rem(rep + t + 1, copies)

    def signal(where):
        pl.semaphore_signal(barrier, inc=1, device_id=where, device_id_type=MESH_ID)

    repeat(domains - 1, lambda t: signal({"dom": dom_peer(t)}))
    repeat(copies - 1, lambda t: signal({"rep": rep_peer(t)}))
    pl.semaphore_wait(barrier, domains + copies - 2)

    def copy(src, dst, send, recv, where):
        return pltpu.make_async_remote_copy(
            src_ref=src,
            dst_ref=dst,
            send_sem=send,
            recv_sem=recv,
            device_id=where,
            device_id_type=MESH_ID,
        )

    def node_copy(t):
        block = nodes_ref.at[pl.ds(pl.multiple_of(dom_peer(t) * size, 8), size)]
        return copy(
            block, landed.at[t], send_sem.at[t], recv_sem.at[t], {"dom": dom_peer(t)}
        )

    def row_copy(t):
        return copy(
            rows_ref, landed_rows.at[t], send_row.at[t], recv_row.at[t], {"rep": rep_peer(t)}
        )

    def total_copy(t):
        return copy(
            total, landed_total.at[t], send_total.at[t], recv_total.at[t], {"rep": rep_peer(t)}
        )

    repeat(domains - 1, lambda t: node_copy(t).start())
    repeat(copies - 1, lambda t: row_copy(t).start())

    repeat(domains - 1, lambda t: node_copy(t).wait_recv())
    mine = nodes_ref[pl.ds(pl.multiple_of(me * size, 8), size), :]
    if domains <= 16:
        for t in range(domains - 1):
            mine = mine + landed[t]
    else:
        mine = lax.fori_loop(0, domains - 1, lambda t, s: s + landed[t], mine)
    total[...] = mine
    repeat(copies - 1, lambda t: row_copy(t).wait_recv())
    rows = rows_ref[...]
    for t in range(copies - 1):
        rows = rows + landed_rows[t]
    rows_out[...] = rows
    repeat(copies - 1, lambda t: total_copy(t).start())
    repeat(domains - 1, lambda t: node_copy(t).wait_send())
    repeat(copies - 1, lambda t: row_copy(t).wait_send())
    repeat(copies - 1, lambda t: total_copy(t).wait_recv())
    for t in range(copies - 1):
        mine = mine + landed_total[t]
    nodes_out[...] = mine
    repeat(copies - 1, lambda t: total_copy(t).wait_send())


def finish_kernel(nodes_ref, rows_ref, normal_ref, order_ref, corner_ref, out_ref):
    node_buckets = nodes_ref.shape[0] // 3
    facet_buckets = rows_ref.shape[0]
    high_at = lax.broadcasted_iota(jnp.int32, (node_buckets, BUCKET), 0)
    low_at = lax.broadcasted_iota(jnp.int32, (BUCKET, BUCKET), 0)
    result = jnp.zeros((6 * node_buckets, BUCKET), F32)

    def spread(index, values, result):
        high = lax.div(index, BUCKET)
        low = index - high * BUCKET
        hit = high == high_at
        onehot = jnp.where(low == low_at, 1.0, 0.0).astype(BF16)
        firsts = [v.astype(BF16).astype(F32) for v in values]
        rests = [v - f for v, f in zip(values, firsts)]
        left = jnp.concatenate([jnp.where(hit, v, 0.0) for v in firsts + rests], 0)
        return result + lax.dot_general(
            left.astype(BF16), onehot, (((1,), (1,)), ((), ())), preferred_element_type=F32
        )

    for j in range(node_buckets):
        values = [
            STIFFNESS * nodes_ref[k * node_buckets + j : k * node_buckets + j + 1, :]
            for k in range(3)
        ]
        result = spread(order_ref[:, j * BUCKET : (j + 1) * BUCKET], values, result)
    for b in range(facet_buckets):
        at = slice(b * BUCKET, (b + 1) * BUCKET)
        row = (-STIFFNESS / 3.0) * rows_ref[b : b + 1, :]
        values = [normal_ref[k : k + 1, at] * row for k in range(3)]
        for corner in range(3):
            result = spread(corner_ref[corner : corner + 1, at], values, result)

    half = 3 * node_buckets
    force = result[:half] + result[half:]
    for k in range(3):
        for h in range(node_buckets):
            i = k * node_buckets + h
            out_ref[k : k + 1, h * BUCKET : (h + 1) * BUCKET] = force[i : i + 1]


def per_device(
    node_pos,
    node_order,
    facet_centroid,
    facet_normal,
    facet_nodes,
    pair_bucket,
    pair_owner,
    pair_slot,
    pair_count,
):
    domains = lax.axis_size("dom")
    copies = lax.axis_size("rep")
    node_buckets = node_pos.shape[1] // BUCKET
    facet_buckets = facet_centroid.shape[1] // BUCKET
    size = 3 * node_buckets
    dma = pltpu.SemaphoreType.DMA
    shape = jax.ShapeDtypeStruct

    points = pl.pallas_call(
        functools.partial(gather_kernel, domains),
        name="gather_points",
        out_shape=shape((domains * size, BUCKET), F32),
        in_specs=[VMEM] * 2,
        out_specs=VMEM,
        scratch_shapes=[dma((domains - 1,)), dma((domains - 1,))],
        compiler_params=pltpu.CompilerParams(collective_id=0, has_side_effects=True),
    )(node_pos, node_order)

    nodes, rows = pl.pallas_call(
        functools.partial(pair_kernel, node_buckets),
        name="pair_forces",
        out_shape=[
            shape(((domains + 1) * size, BUCKET), F32),
            shape((facet_buckets, BUCKET), F32),
        ],
        in_specs=[SMEM] * 4 + [VMEM] * 3,
        out_specs=[VMEM] * 2,
        scratch_shapes=[
            pltpu.VMEM((facet_buckets, 2 * BUCKET, BUCKET), BF16),
            pltpu.VMEM((facet_buckets, 3, BUCKET, BUCKET), F32),
            pltpu.VMEM((facet_buckets + 1, BUCKET, BUCKET), F32),
        ],
    )(
        pair_count,
        pair_bucket.reshape(-1),
        pair_owner.reshape(-1),
        pair_slot.reshape(-1),
        points,
        facet_centroid,
        facet_normal,
    )

    nodes, rows = pl.pallas_call(
        functools.partial(exchange_kernel, domains, copies),
        name="exchange_forces",
        out_shape=[shape((size, BUCKET), F32), shape((facet_buckets, BUCKET), F32)],
        in_specs=[VMEM] * 2,
        out_specs=[VMEM] * 2,
        scratch_shapes=[
            pltpu.VMEM((domains - 1, size, BUCKET), F32),
            pltpu.VMEM((copies - 1, facet_buckets, BUCKET), F32),
            pltpu.VMEM((size, BUCKET), F32),
            pltpu.VMEM((copies - 1, size, BUCKET), F32),
            dma((domains - 1,)),
            dma((domains - 1,)),
            dma((copies - 1,)),
            dma((copies - 1,)),
            dma((copies - 1,)),
            dma((copies - 1,)),
        ],
        compiler_params=pltpu.CompilerParams(collective_id=1, has_side_effects=True),
    )(nodes, rows)

    return pl.pallas_call(
        finish_kernel,
        name="finish_forces",
        out_shape=shape(node_pos.shape, F32),
        in_specs=[VMEM] * 5,
        out_specs=VMEM,
    )(nodes, rows, facet_normal, node_order, facet_nodes)


def solution(mesh):
    placed = (
        P(None, "dom"),
        P("dom", None),
        P(None, "dom"),
        P(None, "dom"),
        P(None, "dom"),
        P("rep", "dom", None),
        P("rep", "dom", None, None),
        P("rep", "dom", None),
        P("rep", "dom"),
    )
    return jax.shard_map(
        per_device, mesh=mesh, in_specs=placed, out_specs=P(None, "dom"), check_vma=False
    )
```

time: 216 us -> 51.3 us (0.24)
  other arithmetic: 85.8 us -> 0 us
  blocking collectives: 55 us -> 0 us
  Pallas kernels: 0 us -> 51 us
  starting transfers between devices: 42.2 us -> 0 us
  local copies, waits for them, and re-layouts: 13.6 us -> 0 us
  waiting for transfers between devices: 12.4 us -> 0 us
  matrix products: 4.18 us -> 0 us
    scatter-add x21 -> x0, other arithmetic: 68.8 us -> none  [the longest x3 35.8 us: per_device(): node_force = node_force.at[:, facet_nodes[corner]].add(reaction)]
    pallas_call x0 -> x4, Pallas kernels: none -> 51 us  [the longest x1 22.3 us: per_device(): pl.pallas_call(functools.partial(exchange_kernel, domains, copies), name=...]
    all_to_all x2 -> x0, starting transfers between devices: 42.2 us -> none  [the longest x1 35.8 us: per_device(): lax.all_to_all(slot_acc[:-1].reshape(domains, per_owner, 3, width), 'dom'...]
    psum x1 -> x0, blocking collectives: 40.3 us -> none  [per_device(): return lax.psum(node_force, 'rep')]
    all_gather x1 -> x0, blocking collectives: 14.8 us -> none  [per_device(): every_bucket = lax.all_gather(bucket_points, 'dom', axis=0, tiled=True)]
    reduce_sum x18 -> x0, other arithmetic: 13.5 us -> none  [the longest x8 8.29 us: tile_terms(): gap = jnp.sum(normal[:, :, :, None] * delta, axis=1)]
    all_to_all x2 -> x0, waiting for transfers between devices: 12.4 us -> none  [the longest x1 12.4 us: per_device(): lax.all_to_all(slot_acc[:-1].reshape(domains, per_owner, 3, width), 'dom'...]
    gather x3 -> x0, local copies, waits for them, and re-layouts: 6.98 us -> none  [the longest x1 5.47 us: per_device(): node_pos[:, node_order[0]].reshape(3, node_buckets, width)]
  transfers between devices with their start and end apart: 2 -> 0, of which waited for: 1 -> 0; matrix products, arithmetic and copies ran while one was open for 20% -> 0% of each run, Pallas kernels for 0% -> 0%
where the time goes in v1:
time: 51.3 us; the launch traced here: 51.6 us
  Pallas kernels  51 us (99%)
  between operations  0.67 us (1%)
    pallas_call x1, Pallas kernels, per_device(): pl.pallas_call(functools.partial(exchange_kernel, domains, copies), name=...  22.3 us
    pallas_call x1, Pallas kernels, per_device(): pl.pallas_call(functools.partial(pair_kernel, node_buckets), name='pair_f...  14.8 us
    pallas_call x1, Pallas kernels, per_device(): pl.pallas_call(functools.partial(gather_kernel, domains), name='gather_po...  10.8 us
    pallas_call x1, Pallas kernels, per_device(): pl.pallas_call(finish_kernel, name='finish_forces', out_shape=shape(node_...  3.03 us

profile of v1, /device:TPU:0, one launch (start us, length us, event | category | flops | bytes accessed | tf_op | source)
XLA Modules:
  0.0 51.6 jit_solution(13744669091140610212)
XLA Ops:
  0.7 10.8 %gather_points.1.points_ref = f32[384,128]{1,0:T(8,128)} custom-call(f32[3,2048]{1,0:T(4,128)} %pos_ref.1, s32[1,2048]{1,0:T(1,128)} %order_ref.3), custom_call_target="tpu_custom_call" | custom-call | tf_op jit(solution)/shard_map/gather_points/pallas_call | solution.py:336
  11.4 14.8 %pair_forces.1 = (f32[432,128]{1,0:T(8,128)}, f32[16,128]{1,0:T(8,128)}) custom-call(s32[1,1]{1,0:T(1,128)S(6)} %copy.10.count_ref, s32[128]{0:T(128)} %bitcast.3, s32[128]{0:T(128)} %bitcast.4, s32[128]{0:T(128)} %bitcast.5, f32[384,128]{1,0:T(8,128)} %gather_points.1.points_ref, f32[3,2048]{1,0:T(4,128)} %centre_ref.1, f32[3,2048]{1,0:T(4,128)} %normal_ref.3), custom_call_target="tpu_custom_call" | custom-call | tf_op jit(solution)/shard_map/pair_forces/pallas_call | solution.py:346
  26.3 22.3 %exchange_forces.1 = (f32[48,128]{1,0:T(8,128)}, f32[16,128]{1,0:T(8,128)}) custom-call(f32[432,128]{1,0:T(8,128)} %get-tuple-element.9.nodes_ref, f32[16,128]{1,0:T(8,128)} %get-tuple-element.10.rows_ref), custom_call_target="tpu_custom_call" | custom-call | tf_op jit(solution)/shard_map/exchange_forces/pallas_call | solution.py:370
  48.6 3.0 %finish_forces.1 = f32[3,2048]{1,0:T(4,128)} custom-call(f32[48,128]{1,0:T(8,128)} %get-tuple-element.11.nodes_ref, f32[16,128]{1,0:T(8,128)} %get-tuple-element.12.rows_ref, f32[3,2048]{1,0:T(4,128)} %normal_ref.3, s32[1,2048]{1,0:T(1,128)} %order_ref.3, s32[3,2048]{1,0:T(4,128)} %corner_ref.1), custom_call_target="tpu_custom_call" | custom-call | tf_op jit(solution)/shard_map/finish_forces/pallas_call | solution.py:391

commit v2 on v1

v2 whole, which is shorter than its diff:
```python
import functools

import jax
import jax.numpy as jnp
from jax import lax
from jax.experimental import pallas as pl
from jax.experimental.pallas import tpu as pltpu
from jax.sharding import PartitionSpec as P

BUCKET = 128
STIFFNESS = 0.125
RADIUS_SQ = 4.0
LOG2E = 1.4426950408889634
MESH_ID = pl.DeviceIdType.MESH
VMEM = pl.BlockSpec(memory_space=pltpu.VMEM)
SMEM = pl.BlockSpec(memory_space=pltpu.SMEM)
F32 = jnp.float32
BF16 = jnp.bfloat16


def repeat(count, body):
    if count <= 16:
        for i in range(count):
            body(i)
    else:
        def step(i, carry):
            body(i)
            return carry

        lax.fori_loop(0, count, step, 0)


def split3(value):
    first = value.astype(BF16).astype(F32)
    rest = value - first
    second = rest.astype(BF16).astype(F32)
    return first, second, rest - second


def facet_tables(centre_ref, normal_ref, geom_ref, wide_ref):
    scale = LOG2E / RADIUS_SQ
    nothing = jnp.zeros((1, BUCKET), F32)

    def prepare(b, carry):
        at = pl.ds(pl.multiple_of(b * BUCKET, BUCKET), BUCKET)
        n = [normal_ref[k : k + 1, at] for k in range(3)]
        c = [centre_ref[k : k + 1, at] for k in range(3)]
        n_c = n[0] * c[0] + n[1] * c[1] + n[2] * c[2]
        c_c = c[0] * c[0] + c[1] * c[1] + c[2] * c[2]
        gap = jnp.concatenate([-n[0], -n[1], -n[2], nothing, n_c] + [nothing] * 3, 0)
        dist = jnp.concatenate(
            [2.0 * scale * c[0], 2.0 * scale * c[1], 2.0 * scale * c[2]]
            + [nothing - scale, -scale * c_c] + [nothing] * 3,
            0,
        )
        raw = jnp.concatenate(n + [nothing] * 5, 0)
        blank = jnp.zeros((BUCKET - 56, BUCKET), F32)
        for part, rows in enumerate((gap, dist)):
            a, bb, cc = split3(rows)
            table = jnp.concatenate([a, bb, cc, a, bb, a, raw, blank], 0).T
            geom_ref[b, part * BUCKET : (part + 1) * BUCKET, :] = table.astype(BF16)
            if part == 0:
                for k in range(3):
                    wide_ref[b, k] = jnp.broadcast_to(table[:, 48 + k : 49 + k], (BUCKET, BUCKET))
        return carry

    lax.fori_loop(0, geom_ref.shape[0], prepare, 0)


def gather_kernel(
    domains,
    pos_ref,
    order_ref,
    centre_ref,
    normal_ref,
    out_ref,
    geom_ref,
    wide_ref,
    send_sem,
    recv_sem,
):
    me = lax.axis_index("dom")
    rows = out_ref.shape[0] // domains
    buckets = rows // 3
    barrier = pltpu.get_barrier_semaphore()

    def greet(t):
        peer = lax.rem(me + t + 1, domains)
        pl.semaphore_signal(barrier, inc=1, device_id={"dom": peer}, device_id_type=MESH_ID)

    repeat(domains - 1, greet)

    order = jnp.concatenate(
        [order_ref[:, h * BUCKET : (h + 1) * BUCKET] for h in range(buckets)], 0
    )
    high = lax.div(order, BUCKET)
    low = order - high * BUCKET
    own = pl.multiple_of(me * rows, 8)
    for k in range(3):
        picked = jnp.zeros((buckets, BUCKET), F32)
        for h in range(buckets):
            row = jnp.broadcast_to(
                pos_ref[k : k + 1, h * BUCKET : (h + 1) * BUCKET], (buckets, BUCKET)
            )
            found = jnp.take_along_axis(row, low, axis=1, mode="promise_in_bounds")
            picked = jnp.where(high == h, found, picked)
        out_ref[pl.ds(own + k * buckets, buckets), :] = picked

    pl.semaphore_wait(barrier, domains - 1)
    block = out_ref.at[pl.ds(own, rows)]

    def copy_to(t):
        peer = lax.rem(me + t + 1, domains)
        return pltpu.make_async_remote_copy(
            src_ref=block,
            dst_ref=block,
            send_sem=send_sem.at[t],
            recv_sem=recv_sem.at[t],
            device_id={"dom": peer},
            device_id_type=MESH_ID,
        )

    def copy_from(t):
        source = lax.rem(me + 2 * domains - t - 1, domains)
        landed = out_ref.at[pl.ds(pl.multiple_of(source * rows, 8), rows)]
        return pltpu.make_async_remote_copy(
            src_ref=landed,
            dst_ref=landed,
            send_sem=send_sem.at[t],
            recv_sem=recv_sem.at[t],
            device_id={"dom": source},
            device_id_type=MESH_ID,
        )

    repeat(domains - 1, lambda t: copy_to(t).start())
    facet_tables(centre_ref, normal_ref, geom_ref, wide_ref)
    repeat(domains - 1, lambda t: copy_from(t).wait_recv())
    repeat(domains - 1, lambda t: copy_to(t).wait_send())


def pair_kernel(
    node_buckets,
    count_ref,
    bucket_ref,
    owner_ref,
    slot_ref,
    points_ref,
    geom_ref,
    wide_ref,
    nodes_ref,
    rows_ref,
    odd_ref,
    even_sum,
    odd_sum,
    even_part,
    odd_part,
):
    facet_buckets = geom_ref.shape[0]
    slots = bucket_ref.shape[0]
    for ref in (nodes_ref, odd_ref, even_sum, odd_sum):
        ref[...] = jnp.zeros_like(ref)

    count = count_ref[0, 0]
    place = lax.broadcasted_iota(jnp.int32, (8, BUCKET), 0)
    blank = jnp.zeros((BUCKET - 48, BUCKET), F32)
    one_or_zero = jnp.where(place == 4, 1.0, 0.0)
    spare = nodes_ref.shape[0] - 3 * node_buckets

    def base_of(p):
        return owner_ref[p] * (3 * node_buckets) + slot_ref[p]

    def products(p, part_ref):
        base = base_of(p)
        x, y, z = (
            jnp.broadcast_to(points_ref[pl.ds(base + k * node_buckets, 1), :], (8, BUCKET))
            for k in range(3)
        )
        square = x * x + y * y + z * z
        value = jnp.where(place == 3, square, one_or_zero)
        value = jnp.where(place == 2, z, value)
        value = jnp.where(place == 1, y, value)
        value = jnp.where(place == 0, x, value)
        v1, v2, v3 = split3(value)
        table = jnp.concatenate([v1, v1, v1, v2, v2, v3, blank], 0).astype(BF16)
        part_ref[...] = jnp.dot(geom_ref[bucket_ref[p]], table, preferred_element_type=F32)

    def forces(p, part_ref, force_ref, sum_ref):
        live = p < count
        at = jnp.minimum(p, slots - 1)
        b = bucket_ref[at]
        minus_gap, fade = part_ref[:BUCKET], part_ref[BUCKET:]
        small = jnp.exp(-jnp.abs(minus_gap))
        logs = jnp.where(small < 2.0**-8, small * (1.0 - 0.5 * small), jnp.log(1.0 + small))
        strength = (jnp.maximum(minus_gap, 0.0) + logs) * jnp.exp2(fade)
        to_bucket = jnp.where(live, b, facet_buckets)
        to_node = jnp.where(live, base_of(at), spare)
        sum_ref[to_bucket] += strength
        for k in range(3):
            term = jnp.sum(wide_ref[b, k] * strength, axis=0, keepdims=True)
            force_ref[pl.ds(to_node + k * node_buckets, 1), :] += term

    products(0, even_part)

    def step(i, carry):
        p = 2 * i
        last = slots - 1
        products(jnp.minimum(p + 1, last), odd_part)
        forces(p, even_part, nodes_ref, even_sum)
        products(jnp.minimum(p + 2, last), even_part)
        forces(p + 1, odd_part, odd_ref, odd_sum)
        return carry

    lax.fori_loop(0, lax.div(count + 1, 2), step, 0)

    nodes_ref[...] += odd_ref[...]
    for b in range(facet_buckets):
        rows_ref[b : b + 1, :] = jnp.sum((even_sum[b] + odd_sum[b]).T, axis=0, keepdims=True)


def spread(index, values, result):
    node_buckets = result.shape[0] // 6
    high_at = lax.broadcasted_iota(jnp.int32, (node_buckets, BUCKET), 0)
    low_at = lax.broadcasted_iota(jnp.int32, (BUCKET, BUCKET), 0)
    high = lax.div(index, BUCKET)
    low = index - high * BUCKET
    hit = high == high_at
    onehot = jnp.where(low == low_at, 1.0, 0.0).astype(BF16)
    firsts = [v.astype(BF16).astype(F32) for v in values]
    rests = [v - f for v, f in zip(values, firsts)]
    left = jnp.concatenate([jnp.where(hit, v, 0.0) for v in firsts + rests], 0)
    return result + lax.dot_general(
        left.astype(BF16), onehot, (((1,), (1,)), ((), ())), preferred_element_type=F32
    )


def exchange_kernel(
    domains,
    copies,
    nodes_ref,
    rows_ref,
    normal_ref,
    order_ref,
    corner_ref,
    out_ref,
    landed,
    total,
    landed_total,
    send_sem,
    recv_sem,
    send_total,
    recv_total,
):
    me = lax.axis_index("dom")
    rep = lax.axis_index("rep")
    size = landed.shape[1]
    node_buckets = size // 3
    facet_buckets = rows_ref.shape[0]
    barrier = pltpu.get_barrier_semaphore()

    def dom_peer(t):
        return lax.rem(me + t + 1, domains)

    def rep_peer(t):
        return lax.rem(rep + t + 1, copies)

    def signal(where):
        pl.semaphore_signal(barrier, inc=1, device_id=where, device_id_type=MESH_ID)

    repeat(domains - 1, lambda t: signal({"dom": dom_peer(t)}))
    repeat(copies - 1, lambda t: signal({"rep": rep_peer(t)}))
    pl.semaphore_wait(barrier, domains + copies - 2)

    def copy(src, dst, send, recv, where):
        return pltpu.make_async_remote_copy(
            src_ref=src,
            dst_ref=dst,
            send_sem=send,
            recv_sem=recv,
            device_id=where,
            device_id_type=MESH_ID,
        )

    def node_copy(t):
        block = nodes_ref.at[pl.ds(pl.multiple_of(dom_peer(t) * size, 8), size)]
        return copy(
            block, landed.at[t], send_sem.at[t], recv_sem.at[t], {"dom": dom_peer(t)}
        )

    def total_copy(t):
        return copy(
            total, landed_total.at[t], send_total.at[t], recv_total.at[t], {"rep": rep_peer(t)}
        )

    repeat(domains - 1, lambda t: node_copy(t).start())

    result = jnp.zeros((2 * size, BUCKET), F32)
    for b in range(facet_buckets):
        at = slice(b * BUCKET, (b + 1) * BUCKET)
        row = (-STIFFNESS / 3.0) * rows_ref[b : b + 1, :]
        values = [normal_ref[k : k + 1, at] * row for k in range(3)]
        for corner in range(3):
            result = spread(corner_ref[corner : corner + 1, at], values, result)

    repeat(domains - 1, lambda t: node_copy(t).wait_recv())
    mine = nodes_ref[pl.ds(pl.multiple_of(me * size, 8), size), :]
    if domains <= 16:
        for t in range(domains - 1):
            mine = mine + landed[t]
    else:
        mine = lax.fori_loop(0, domains - 1, lambda t, s: s + landed[t], mine)
    mine = STIFFNESS * mine
    for j in range(node_buckets):
        values = [
            mine[k * node_buckets + j : k * node_buckets + j + 1, :] for k in range(3)
        ]
        result = spread(order_ref[:, j * BUCKET : (j + 1) * BUCKET], values, result)
    force = result[:size] + result[size:]
    total[...] = force
    repeat(domains - 1, lambda t: node_copy(t).wait_send())
    repeat(copies - 1, lambda t: total_copy(t).start())
    repeat(copies - 1, lambda t: total_copy(t).wait_recv())
    for t in range(copies - 1):
        force = force + landed_total[t]
    for k in range(3):
        for h in range(node_buckets):
            i = k * node_buckets + h
            out_ref[k : k + 1, h * BUCKET : (h + 1) * BUCKET] = force[i : i + 1]
    repeat(copies - 1, lambda t: total_copy(t).wait_send())


def per_device(
    node_pos,
    node_order,
    facet_centroid,
    facet_normal,
    facet_nodes,
    pair_bucket,
    pair_owner,
    pair_slot,
    pair_count,
):
    domains = lax.axis_size("dom")
    copies = lax.axis_size("rep")
    node_buckets = node_pos.shape[1] // BUCKET
    facet_buckets = facet_centroid.shape[1] // BUCKET
    size = 3 * node_buckets
    dma = pltpu.SemaphoreType.DMA
    shape = jax.ShapeDtypeStruct

    points, geom, wide = pl.pallas_call(
        functools.partial(gather_kernel, domains),
        name="gather_points",
        out_shape=[
            shape((domains * size, BUCKET), F32),
            shape((facet_buckets, 2 * BUCKET, BUCKET), BF16),
            shape((facet_buckets, 3, BUCKET, BUCKET), F32),
        ],
        in_specs=[VMEM] * 4,
        out_specs=[VMEM] * 3,
        scratch_shapes=[dma((domains - 1,)), dma((domains - 1,))],
        compiler_params=pltpu.CompilerParams(
            collective_id=0, has_side_effects=True, vmem_limit_bytes=16 << 20
        ),
    )(node_pos, node_order, facet_centroid, facet_normal)

    nodes, rows = pl.pallas_call(
        functools.partial(pair_kernel, node_buckets),
        name="pair_forces",
        out_shape=[
            shape(((domains + 1) * size, BUCKET), F32),
            shape((facet_buckets, BUCKET), F32),
        ],
        in_specs=[SMEM] * 4 + [VMEM] * 3,
        out_specs=[VMEM] * 2,
        scratch_shapes=[
            pltpu.VMEM(((domains + 1) * size, BUCKET), F32),
            pltpu.VMEM((facet_buckets + 1, BUCKET, BUCKET), F32),
            pltpu.VMEM((facet_buckets + 1, BUCKET, BUCKET), F32),
            pltpu.VMEM((2 * BUCKET, BUCKET), F32),
            pltpu.VMEM((2 * BUCKET, BUCKET), F32),
        ],
        compiler_params=pltpu.CompilerParams(vmem_limit_bytes=32 << 20),
    )(
        pair_count,
        pair_bucket.reshape(-1),
        pair_owner.reshape(-1),
        pair_slot.reshape(-1),
        points,
        geom,
        wide,
    )

    return pl.pallas_call(
        functools.partial(exchange_kernel, domains, copies),
        name="exchange_forces",
        out_shape=shape(node_pos.shape, F32),
        in_specs=[VMEM] * 5,
        out_specs=VMEM,
        scratch_shapes=[
            pltpu.VMEM((domains - 1, size, BUCKET), F32),
            pltpu.VMEM((size, BUCKET), F32),
            pltpu.VMEM((copies - 1, size, BUCKET), F32),
            dma((domains - 1,)),
            dma((domains - 1,)),
            dma((copies - 1,)),
            dma((copies - 1,)),
        ],
        compiler_params=pltpu.CompilerParams(
            collective_id=1, has_side_effects=True, vmem_limit_bytes=16 << 20
        ),
    )(nodes, rows, facet_normal, node_order, facet_nodes)


def solution(mesh):
    placed = (
        P(None, "dom"),
        P("dom", None),
        P(None, "dom"),
        P(None, "dom"),
        P(None, "dom"),
        P("rep", "dom", None),
        P("rep", "dom", None, None),
        P("rep", "dom", None),
        P("rep", "dom"),
    )
    return jax.shard_map(
        per_device, mesh=mesh, in_specs=placed, out_specs=P(None, "dom"), check_vma=False
    )
```

time: 51.3 us -> 44.2 us (0.86); the launches traced: 51.6 us -> 43.7 us
  Pallas kernels: 51 us -> 37.4 us
  local copies, waits for them, and re-layouts: 0 us -> 5.55 us
    pallas_call x1, Pallas kernels: 22.3 us -> 12.8 us  [per_device(): pl.pallas_call(functools.partial(exchange_kernel, domains, copies), name=...]
    unnamed x0 -> x21, local copies, waits for them, and re-layouts: none -> 5.55 us
    pallas_call x1 -> x0, Pallas kernels: 3.03 us -> none  [per_device(): pl.pallas_call(finish_kernel, name='finish_forces', out_shape=shape(node_...]
    pallas_call x1, Pallas kernels: 10.8 us -> 9.57 us  [per_device(): pl.pallas_call(functools.partial(gather_kernel, domains), name='gather_po...]
where the time goes in v2:
time: 44.2 us; the launch traced here: 43.7 us
  Pallas kernels  37.4 us (85%)
  local copies, waits for them, and re-layouts  5.55 us (13%)
  between operations  0.72 us (2%)
    pallas_call x1, Pallas kernels, per_device(): pl.pallas_call(functools.partial(pair_kernel, node_buckets), name='pair_f...  15.1 us
    pallas_call x1, Pallas kernels, per_device(): pl.pallas_call(functools.partial(exchange_kernel, domains, copies), name=...  12.8 us
    pallas_call x1, Pallas kernels, per_device(): pl.pallas_call(functools.partial(gather_kernel, domains), name='gather_po...  9.57 us
    unnamed x21, local copies, waits for them, and re-layouts  5.55 us

profile of v2, /device:TPU:0, one launch (start us, length us, event | category | flops | bytes accessed | tf_op | source)
XLA Modules:
  0.0 43.7 jit_solution(583518980921965935)
XLA Ops:
  0.7 0.0 copy-start
  0.7 0.7 %copy-done = f32[3,2048]{1,0:T(4,128)S(1)} copy-done((f32[3,2048]{1,0:T(4,128)S(1)}, f32[3,2048]{1,0:T(4,128)}, u32[]{:S(2)}) %copy-start) | copy-done | bytes 24600
  1.4 0.0 copy-start.2
  1.4 0.8 %copy-done.2 = f32[3,2048]{1,0:T(4,128)S(1)} copy-done((f32[3,2048]{1,0:T(4,128)S(1)}, f32[3,2048]{1,0:T(4,128)}, u32[]{:S(2)}) %copy-start.2) | copy-done | bytes 24600
  2.2 0.0 copy-start.3
  2.2 0.8 %copy-done.3 = f32[3,2048]{1,0:T(4,128)S(1)} copy-done((f32[3,2048]{1,0:T(4,128)S(1)}, f32[3,2048]{1,0:T(4,128)}, u32[]{:S(2)}) %copy-start.3) | copy-done | bytes 24600
  2.9 0.0 copy-start.5
  2.9 0.7 %copy-done.5 = s32[1,2048]{1,0:T(1,128)S(1)} copy-done((s32[1,2048]{1,0:T(1,128)S(1)}, s32[1,2048]{1,0:T(1,128)}, u32[]{:S(2)}) %copy-start.5) | copy-done | bytes 8216
  3.6 0.0 copy-start.1
  3.6 0.0 copy-start.4
  3.6 0.0 copy-start.6
  3.6 9.6 %gather_points.1 = (f32[384,128]{1,0:T(8,128)S(1)}, bf16[16,256,128]{2,1,0:T(8,128)(2,1)S(1)}, f32[16,3,128,128]{3,2,1,0:T(8,128)S(1)}) custom-call(f32[3,2048]{1,0:T(4,128)S(1)} %copy-done.2, s32[1,2048]{1,0:T(1,128)S(1)} %copy-done.5, f32[3,2048]{1,0:T(4,128)S(1)} %copy-done.3, f32[3,2048]{1,0:T(4,128)S(1)} %copy-done), custom_call_target="tpu_custom_call" | custom-call | tf_op jit(solution)/shard_map/gather_points/pallas_call | solution.py:350
  13.2 0.0 copy-start.7
  13.2 0.6 %copy-done.7 = s32[1,1,128]{2,1,0:T(1,128)S(1)} copy-done((s32[1,1,128]{2,1,0:T(1,128)S(1)}, s32[1,1,128]{2,1,0:T(1,128)}, u32[]{:S(2)}) %copy-start.7) | copy-done | bytes 536
  13.9 0.0 copy-start.8
  13.9 0.7 %copy-done.8 = s32[1,1,128,1]{2,3,1,0:T(1,128)S(1)} copy-done((s32[1,1,128,1]{2,3,1,0:T(1,128)S(1)}, s32[1,1,128,1]{2,3,1,0:T(1,128)}, u32[]{:S(2)}) %copy-start.8) | copy-done | bytes 536
  14.5 0.0 copy-start.9
  14.5 0.7 %copy-done.9 = s32[1,1,128]{2,1,0:T(1,128)S(1)} copy-done((s32[1,1,128]{2,1,0:T(1,128)S(1)}, s32[1,1,128]{2,1,0:T(1,128)}, u32[]{:S(2)}) %copy-start.9) | copy-done | bytes 536
  15.2 15.1 %pair_forces.1 = (f32[432,128]{1,0:T(8,128)S(1)}, f32[16,128]{1,0:T(8,128)S(1)}) custom-call(s32[1,1]{1,0:T(1,128)S(6)} %copy.11.count_ref, s32[128]{0:T(128)S(1)} %bitcast.3, s32[128]{0:T(128)S(1)} %bitcast.4, s32[128]{0:T(128)S(1)} %bitcast.5, f32[384,128]{1,0:T(8,128)S(1)} %get-tuple-element.10.points_ref, ...), custom_call_target="tpu_custom_call" | custom-call | tf_op jit(solution)/shard_map/pair_forces/pallas_call | solution.py:366
  30.3 0.0 copy-done.1
  30.3 0.0 copy-done.4
  30.3 0.0 copy-done.6
  30.3 12.8 %exchange_forces.1 = f32[3,2048]{1,0:T(4,128)S(1)} custom-call(f32[432,128]{1,0:T(8,128)S(1)} %get-tuple-element.13.nodes_ref, f32[16,128]{1,0:T(8,128)S(1)} %get-tuple-element.14.rows_ref, f32[3,2048]{1,0:T(4,128)S(1)} %copy-done.1, s32[1,2048]{1,0:T(1,128)S(1)} %copy-done.6, s32[3,2048]{1,0:T(4,128)S(1)} %copy-done.4), custom_call_target="tpu_custom_call" | custom-call | tf_op jit(solution)/shard_map/exchange_forces/pallas_call | solution.py:393
  43.1 0.6 %copy.12 = f32[3,2048]{1,0:T(4,128)} copy(f32[3,2048]{1,0:T(4,128)S(1)} %exchange_forces.1) | data formatting | bytes 49152
Async XLA Ops:
  0.7 0.8 %copy-start = (f32[3,2048]{1,0:T(4,128)S(1)}, f32[3,2048]{1,0:T(4,128)}, u32[]{:S(2)}) copy-start(f32[3,2048]{1,0:T(4,128)} %normal_ref.3) | copy-start | bytes 73732
  1.4 0.8 %copy-start.2 = (f32[3,2048]{1,0:T(4,128)S(1)}, f32[3,2048]{1,0:T(4,128)}, u32[]{:S(2)}) copy-start(f32[3,2048]{1,0:T(4,128)} %pos_ref.1) | copy-start | bytes 73732
  2.2 0.8 %copy-start.3 = (f32[3,2048]{1,0:T(4,128)S(1)}, f32[3,2048]{1,0:T(4,128)}, u32[]{:S(2)}) copy-start(f32[3,2048]{1,0:T(4,128)} %centre_ref.1) | copy-start | bytes 73732
  2.9 0.7 %copy-start.5 = (s32[1,2048]{1,0:T(1,128)S(1)}, s32[1,2048]{1,0:T(1,128)}, u32[]{:S(2)}) copy-start(s32[1,2048]{1,0:T(1,128)} %order_ref.3) | copy-start | bytes 24580
  3.6 26.6 %copy-start.1 = (f32[3,2048]{1,0:T(4,128)S(1)}, f32[3,2048]{1,0:T(4,128)}, u32[]{:S(2)}) copy-start(f32[3,2048]{1,0:T(4,128)} %normal_ref.3) | copy-start | bytes 73732
  3.6 26.6 %copy-start.4 = (s32[3,2048]{1,0:T(4,128)S(1)}, s32[3,2048]{1,0:T(4,128)}, u32[]{:S(2)}) copy-start(s32[3,2048]{1,0:T(4,128)} %corner_ref.1) | copy-start | bytes 73732
  3.6 26.7 %copy-start.6 = (s32[1,2048]{1,0:T(1,128)S(1)}, s32[1,2048]{1,0:T(1,128)}, u32[]{:S(2)}) copy-start(s32[1,2048]{1,0:T(1,128)} %order_ref.3) | copy-start | bytes 24580
  13.2 0.7 %copy-start.7 = (s32[1,1,128]{2,1,0:T(1,128)S(1)}, s32[1,1,128]{2,1,0:T(1,128)}, u32[]{:S(2)}) copy-start(s32[1,1,128]{2,1,0:T(1,128)} %param.14) | copy-start | bytes 1540
  13.9 0.7 %copy-start.8 = (s32[1,1,128,1]{2,3,1,0:T(1,128)S(1)}, s32[1,1,128,1]{2,3,1,0:T(1,128)}, u32[]{:S(2)}) copy-start(s32[1,1,128,1]{2,3,1,0:T(1,128)} %param.15) | copy-start | bytes 1540
  14.5 0.7 %copy-start.9 = (s32[1,1,128]{2,1,0:T(1,128)S(1)}, s32[1,1,128]{2,1,0:T(1,128)}, u32[]{:S(2)}) copy-start(s32[1,1,128]{2,1,0:T(1,128)} %param.16) | copy-start | bytes 1540

commit v3 on v2

--- a/solution.py
+++ b/solution.py
@@ -14,6 +14,7 @@
 MESH_ID = pl.DeviceIdType.MESH
 VMEM = pl.BlockSpec(memory_space=pltpu.VMEM)
 SMEM = pl.BlockSpec(memory_space=pltpu.SMEM)
+HBM = pl.BlockSpec(memory_space=pltpu.HBM)
 F32 = jnp.float32
 BF16 = jnp.bfloat16
 
@@ -30,6 +31,15 @@
         lax.fori_loop(0, count, step, 0)
 
 
+def across(me, mask, domains):
+    peer = me
+    bit = 1
+    while bit < domains:
+        peer = peer + bit * ((mask // bit) % 2) * (1 - 2 * ((me // bit) % 2))
+        bit *= 2
+    return peer
+
+
 def split3(value):
     first = value.astype(BF16).astype(F32)
     rest = value - first
@@ -37,7 +47,7 @@
     return first, second, rest - second
 
 
-def facet_tables(centre_ref, normal_ref, geom_ref, wide_ref):
+def facet_tables(centre_ref, normal_ref, geom_ref, wide_ref, begin, end):
     scale = LOG2E / RADIUS_SQ
     nothing = jnp.zeros((1, BUCKET), F32)
 
@@ -54,47 +64,77 @@
             0,
         )
         raw = jnp.concatenate(n + [nothing] * 5, 0)
-        blank = jnp.zeros((BUCKET - 56, BUCKET), F32)
-        for part, rows in enumerate((gap, dist)):
-            a, bb, cc = split3(rows)
-            table = jnp.concatenate([a, bb, cc, a, bb, a, raw, blank], 0).T
-            geom_ref[b, part * BUCKET : (part + 1) * BUCKET, :] = table.astype(BF16)
-            if part == 0:
-                for k in range(3):
-                    wide_ref[b, k] = jnp.broadcast_to(table[:, 48 + k : 49 + k], (BUCKET, BUCKET))
+        blank = jnp.zeros((BUCKET - 104, BUCKET), F32)
+        rows = []
+        for part in (gap, dist):
+            first, second, third = split3(part)
+            rows += [first, second, third, first, second, first]
+        table = jnp.concatenate(rows + [raw, blank], 0).T
+        geom_ref[b] = table.astype(BF16)
+        for k in range(3):
+            wide_ref[b, k] = jnp.broadcast_to(table[:, 96 + k : 97 + k], (BUCKET, BUCKET))
         return carry
 
-    lax.fori_loop(0, geom_ref.shape[0], prepare, 0)
+    lax.fori_loop(begin, end, prepare, 0)
 
 
 def gather_kernel(
     domains,
+    pos_hbm,
+    order_hbm,
+    centre_hbm,
+    normal_hbm,
+    out_ref,
+    geom_ref,
+    wide_ref,
     pos_ref,
     order_ref,
     centre_ref,
     normal_ref,
-    out_ref,
-    geom_ref,
-    wide_ref,
+    load_sem,
     send_sem,
     recv_sem,
 ):
     me = lax.axis_index("dom")
     rows = out_ref.shape[0] // domains
     buckets = rows // 3
+    loads = [
+        pltpu.make_async_copy(src, dst, load_sem.at[i])
+        for i, (src, dst) in enumerate(
+            (
+                (pos_hbm, pos_ref),
+                (order_hbm, order_ref),
+                (centre_hbm, centre_ref),
+                (normal_hbm, normal_ref),
+            )
+        )
+    ]
+    for load in loads:
+        load.start()
     barrier = pltpu.get_barrier_semaphore()
-
-    def greet(t):
-        peer = lax.rem(me + t + 1, domains)
-        pl.semaphore_signal(barrier, inc=1, device_id={"dom": peer}, device_id_type=MESH_ID)
-
-    repeat(domains - 1, greet)
+    far = domains // 2 - 1
+    partner = across(me, 1, domains)
+
+    def far_mask(t):
+        return domains - 2 - 2 * t
+
+    def greet(where):
+        pl.semaphore_signal(barrier, inc=1, device_id={"dom": where}, device_id_type=MESH_ID)
+
+    repeat(far, lambda t: greet(across(me, far_mask(t), domains)))
+    greet(partner)
+    loads[0].wait()
+    loads[1].wait()
 
     order = jnp.concatenate(
         [order_ref[:, h * BUCKET : (h + 1) * BUCKET] for h in range(buckets)], 0
     )
     high = lax.div(order, BUCKET)
     low = order - high * BUCKET
+
+    def block_of(domain):
+        return out_ref.at[pl.ds(pl.multiple_of(domain * rows, 8), rows)]
+
     own = pl.multiple_of(me * rows, 8)
     for k in range(3):
         picked = jnp.zeros((buckets, BUCKET), F32)
@@ -106,49 +146,67 @@
             picked = jnp.where(high == h, found, picked)
         out_ref[pl.ds(own + k * buckets, buckets), :] = picked
 
-    pl.semaphore_wait(barrier, domains - 1)
-    block = out_ref.at[pl.ds(own, rows)]
-
-    def copy_to(t):
-        peer = lax.rem(me + t + 1, domains)
+    pl.semaphore_wait(barrier, far + 1)
+
+    def copy(domain, number, where):
         return pltpu.make_async_remote_copy(
-            src_ref=block,
-            dst_ref=block,
-            send_sem=send_sem.at[t],
-            recv_sem=recv_sem.at[t],
-            device_id={"dom": peer},
+            src_ref=block_of(domain),
+            dst_ref=block_of(domain),
+            send_sem=send_sem.at[number],
+            recv_sem=recv_sem.at[number],
+            device_id={"dom": where},
             device_id_type=MESH_ID,
         )
 
-    def copy_from(t):
-        source = lax.rem(me + 2 * domains - t - 1, domains)
-        landed = out_ref.at[pl.ds(pl.multiple_of(source * rows, 8), rows)]
-        return pltpu.make_async_remote_copy(
-            src_ref=landed,
-            dst_ref=landed,
-            send_sem=send_sem.at[t],
-            recv_sem=recv_sem.at[t],
-            device_id={"dom": source},
-            device_id_type=MESH_ID,
-        )
-
-    repeat(domains - 1, lambda t: copy_to(t).start())
-    facet_tables(centre_ref, normal_ref, geom_ref, wide_ref)
-    repeat(domains - 1, lambda t: copy_from(t).wait_recv())
-    repeat(domains - 1, lambda t: copy_to(t).wait_send())
+    def far_copy(t):
+        return copy(me, t, across(me, far_mask(t), domains))
+
+    def far_landed(t):
+        where = across(me, far_mask(t), domains)
+        return copy(where, t, where)
+
+    def pass_on(t):
+        return copy(across(me, far_mask(t), domains), far + t, partner)
+
+    def passed_landed(t):
+        return copy(across(partner, far_mask(t), domains), far + t, partner)
+
+    repeat(far, lambda t: far_copy(t).start())
+    copy(me, 2 * far, partner).start()
+    loads[2].wait()
+    loads[3].wait()
+    facet_tables(centre_ref, normal_ref, geom_ref, wide_ref, 0, geom_ref.shape[0] // 2)
+
+    def forward(t):
+        far_landed(far - 1 - t).wait_recv()
+        pass_on(far - 1 - t).start()
+
+    repeat(far, forward)
+    facet_tables(
+        centre_ref, normal_ref, geom_ref, wide_ref, geom_ref.shape[0] // 2, geom_ref.shape[0]
+    )
+    repeat(far, lambda t: passed_landed(t).wait_recv())
+    copy(partner, 2 * far, partner).wait_recv()
+    repeat(far, lambda t: far_copy(t).wait_send())
+    repeat(far, lambda t: pass_on(t).wait_send())
+    copy(me, 2 * far, partner).wait_send()
 
 
 def pair_kernel(
     node_buckets,
     count_ref,
-    bucket_ref,
-    owner_ref,
-    slot_ref,
+    bucket_hbm,
+    owner_hbm,
+    slot_hbm,
     points_ref,
     geom_ref,
     wide_ref,
     nodes_ref,
     rows_ref,
+    bucket_ref,
+    owner_ref,
+    slot_ref,
+    load_sem,
     odd_ref,
     even_sum,
     odd_sum,
@@ -157,12 +215,20 @@
 ):
     facet_buckets = geom_ref.shape[0]
     slots = bucket_ref.shape[0]
+    loads = [
+        pltpu.make_async_copy(src, dst, load_sem.at[i])
+        for i, (src, dst) in enumerate(
+            ((bucket_hbm, bucket_ref), (owner_hbm, owner_ref), (slot_hbm, slot_ref))
+        )
+    ]
+    for load in loads:
+        load.start()
     for ref in (nodes_ref, odd_ref, even_sum, odd_sum):
         ref[...] = jnp.zeros_like(ref)
 
     count = count_ref[0, 0]
     place = lax.broadcasted_iota(jnp.int32, (8, BUCKET), 0)
-    blank = jnp.zeros((BUCKET - 48, BUCKET), F32)
+    blank = jnp.zeros((8, BUCKET), F32)
     one_or_zero = jnp.where(place == 4, 1.0, 0.0)
     spare = nodes_ref.shape[0] - 3 * node_buckets
 
@@ -181,14 +247,17 @@
         value = jnp.where(place == 1, y, value)
         value = jnp.where(place == 0, x, value)
         v1, v2, v3 = split3(value)
-        table = jnp.concatenate([v1, v1, v1, v2, v2, v3, blank], 0).astype(BF16)
+        parts = [v1, v1, v1, v2, v2, v3]
+        left = jnp.concatenate(parts + [blank] * 10, 0)
+        right = jnp.concatenate([blank] * 6 + parts + [blank] * 4, 0)
+        table = jnp.concatenate([left, right], 1).astype(BF16)
         part_ref[...] = jnp.dot(geom_ref[bucket_ref[p]], table, preferred_element_type=F32)
 
     def forces(p, part_ref, force_ref, sum_ref):
         live = p < count
         at = jnp.minimum(p, slots - 1)
         b = bucket_ref[at]
-        minus_gap, fade = part_ref[:BUCKET], part_ref[BUCKET:]
+        minus_gap, fade = part_ref[:, :BUCKET], part_ref[:, BUCKET:]
         small = jnp.exp(-jnp.abs(minus_gap))
         logs = jnp.where(small < 2.0**-8, small * (1.0 - 0.5 * small), jnp.log(1.0 + small))
         strength = (jnp.maximum(minus_gap, 0.0) + logs) * jnp.exp2(fade)
@@ -199,6 +268,8 @@
             term = jnp.sum(wide_ref[b, k] * strength, axis=0, keepdims=True)
             force_ref[pl.ds(to_node + k * node_buckets, 1), :] += term
 
+    for load in loads:
+        load.wait()
     products(0, even_part)
 
     def step(i, carry):
@@ -258,7 +329,7 @@
     barrier = pltpu.get_barrier_semaphore()
 
     def dom_peer(t):
-        return lax.rem(me + t + 1, domains)
+        return across(me, domains - 1 - t, domains)
 
     def rep_peer(t):
         return lax.rem(rep + t + 1, copies)
@@ -352,12 +423,20 @@
         name="gather_points",
         out_shape=[
             shape((domains * size, BUCKET), F32),
-            shape((facet_buckets, 2 * BUCKET, BUCKET), BF16),
+            shape((facet_buckets, BUCKET, BUCKET), BF16),
             shape((facet_buckets, 3, BUCKET, BUCKET), F32),
         ],
-        in_specs=[VMEM] * 4,
+        in_specs=[HBM] * 4,
         out_specs=[VMEM] * 3,
-        scratch_shapes=[dma((domains - 1,)), dma((domains - 1,))],
+        scratch_shapes=[
+            pltpu.VMEM(node_pos.shape, F32),
+            pltpu.VMEM(node_order.shape, jnp.int32),
+            pltpu.VMEM(facet_centroid.shape, F32),
+            pltpu.VMEM(facet_normal.shape, F32),
+            dma((4,)),
+            dma((domains - 1,)),
+            dma((domains - 1,)),
+        ],
         compiler_params=pltpu.CompilerParams(
             collective_id=0, has_side_effects=True, vmem_limit_bytes=16 << 20
         ),
@@ -370,14 +449,18 @@
             shape(((domains + 1) * size, BUCKET), F32),
             shape((facet_buckets, BUCKET), F32),
         ],
-        in_specs=[SMEM] * 4 + [VMEM] * 3,
+        in_specs=[SMEM] + [HBM] * 3 + [VMEM] * 3,
         out_specs=[VMEM] * 2,
         scratch_shapes=[
+            pltpu.SMEM((pair_bucket.size,), jnp.int32),
+            pltpu.SMEM((pair_bucket.size,), jnp.int32),
+            pltpu.SMEM((pair_bucket.size,), jnp.int32),
+            dma((3,)),
             pltpu.VMEM(((domains + 1) * size, BUCKET), F32),
             pltpu.VMEM((facet_buckets + 1, BUCKET, BUCKET), F32),
             pltpu.VMEM((facet_buckets + 1, BUCKET, BUCKET), F32),
-            pltpu.VMEM((2 * BUCKET, BUCKET), F32),
-            pltpu.VMEM((2 * BUCKET, BUCKET), F32),
+            pltpu.VMEM((BUCKET, 2 * BUCKET), F32),
+            pltpu.VMEM((BUCKET, 2 * BUCKET), F32),
         ],
         compiler_params=pltpu.CompilerParams(vmem_limit_bytes=32 << 20),
     )(

time: 44.2 us -> 46.6 us (1.054)
  Pallas kernels: 37.4 us -> 39.9 us
    pallas_call x1, Pallas kernels: 15.1 us -> 16.1 us  [per_device(): pl.pallas_call(functools.partial(pair_kernel, node_buckets), name='pair_f...]
    pallas_call x1, Pallas kernels: 9.57 us -> 10.5 us  [per_device(): pl.pallas_call(functools.partial(gather_kernel, domains), name='gather_po...]
    pallas_call x1, Pallas kernels: 12.8 us -> 13.3 us  [per_device(): pl.pallas_call(functools.partial(exchange_kernel, domains, copies), name=...]
where the time goes in v3:
time: 46.6 us; the launch traced here: 46.2 us
  Pallas kernels  39.9 us (86%)
  local copies, waits for them, and re-layouts  5.55 us (12%)
  between operations  0.72 us (2%)
    pallas_call x1, Pallas kernels, per_device(): pl.pallas_call(functools.partial(pair_kernel, node_buckets), name='pair_f...  16.1 us
    pallas_call x1, Pallas kernels, per_device(): pl.pallas_call(functools.partial(exchange_kernel, domains, copies), name=...  13.3 us
    pallas_call x1, Pallas kernels, per_device(): pl.pallas_call(functools.partial(gather_kernel, domains), name='gather_po...  10.5 us
    unnamed x21, local copies, waits for them, and re-layouts  5.55 us

profile of v3, /device:TPU:0, one launch (start us, length us, event | category | flops | bytes accessed | tf_op | source)
XLA Modules:
  0.0 46.2 jit_solution(10144647913462233657)
XLA Ops:
  0.7 0.0 copy-start
  0.7 0.7 %copy-done = f32[3,2048]{1,0:T(4,128)S(1)} copy-done((f32[3,2048]{1,0:T(4,128)S(1)}, f32[3,2048]{1,0:T(4,128)}, u32[]{:S(2)}) %copy-start) | copy-done | bytes 24600
  1.4 0.0 copy-start.2
  1.4 0.8 %copy-done.2 = f32[3,2048]{1,0:T(4,128)S(1)} copy-done((f32[3,2048]{1,0:T(4,128)S(1)}, f32[3,2048]{1,0:T(4,128)}, u32[]{:S(2)}) %copy-start.2) | copy-done | bytes 24600
  2.2 0.0 copy-start.3
  2.2 0.8 %copy-done.3 = f32[3,2048]{1,0:T(4,128)S(1)} copy-done((f32[3,2048]{1,0:T(4,128)S(1)}, f32[3,2048]{1,0:T(4,128)}, u32[]{:S(2)}) %copy-start.3) | copy-done | bytes 24600
  2.9 0.0 copy-start.5
  2.9 0.7 %copy-done.5 = s32[1,2048]{1,0:T(1,128)S(1)} copy-done((s32[1,2048]{1,0:T(1,128)S(1)}, s32[1,2048]{1,0:T(1,128)}, u32[]{:S(2)}) %copy-start.5) | copy-done | bytes 8216
  3.6 0.0 copy-start.1
  3.6 0.0 copy-start.4
  3.6 0.0 copy-start.6
  3.6 10.5 %gather_points.1 = (f32[384,128]{1,0:T(8,128)S(1)}, bf16[16,128,128]{2,1,0:T(8,128)(2,1)S(1)}, f32[16,3,128,128]{3,2,1,0:T(8,128)S(1)}) custom-call(f32[3,2048]{1,0:T(4,128)S(1)} %copy-done.2, s32[1,2048]{1,0:T(1,128)S(1)} %copy-done.5, f32[3,2048]{1,0:T(4,128)S(1)} %copy-done.3, f32[3,2048]{1,0:T(4,128)S(1)} %copy-done), custom_call_target="tpu_custom_call" | custom-call | tf_op jit(solution)/shard_map/gather_points/pallas_call | solution.py:421
  14.1 0.0 copy-start.7
  14.1 0.6 %copy-done.7 = s32[1,1,128]{2,1,0:T(1,128)S(1)} copy-done((s32[1,1,128]{2,1,0:T(1,128)S(1)}, s32[1,1,128]{2,1,0:T(1,128)}, u32[]{:S(2)}) %copy-start.7) | copy-done | bytes 536
  14.8 0.0 copy-start.8
  14.8 0.7 %copy-done.8 = s32[1,1,128,1]{2,3,1,0:T(1,128)S(1)} copy-done((s32[1,1,128,1]{2,3,1,0:T(1,128)S(1)}, s32[1,1,128,1]{2,3,1,0:T(1,128)}, u32[]{:S(2)}) %copy-start.8) | copy-done | bytes 536
  15.4 0.0 copy-start.9
  15.4 0.7 %copy-done.9 = s32[1,1,128]{2,1,0:T(1,128)S(1)} copy-done((s32[1,1,128]{2,1,0:T(1,128)S(1)}, s32[1,1,128]{2,1,0:T(1,128)}, u32[]{:S(2)}) %copy-start.9) | copy-done | bytes 536
  16.1 16.1 %pair_forces.1 = (f32[432,128]{1,0:T(8,128)S(1)}, f32[16,128]{1,0:T(8,128)S(1)}) custom-call(s32[1,1]{1,0:T(1,128)S(6)} %copy.11.count_ref, s32[128]{0:T(128)S(1)} %bitcast.3, s32[128]{0:T(128)S(1)} %bitcast.4, s32[128]{0:T(128)S(1)} %bitcast.5, f32[384,128]{1,0:T(8,128)S(1)} %get-tuple-element.10.points_ref, ...), custom_call_target="tpu_custom_call" | custom-call | tf_op jit(solution)/shard_map/pair_forces/pallas_call | solution.py:445
  32.2 0.0 copy-done.1
  32.2 0.0 copy-done.4
  32.2 0.0 copy-done.6
  32.2 13.3 %exchange_forces.1 = f32[3,2048]{1,0:T(4,128)S(1)} custom-call(f32[432,128]{1,0:T(8,128)S(1)} %get-tuple-element.13.nodes_ref, f32[16,128]{1,0:T(8,128)S(1)} %get-tuple-element.14.rows_ref, f32[3,2048]{1,0:T(4,128)S(1)} %copy-done.1, s32[1,2048]{1,0:T(1,128)S(1)} %copy-done.6, s32[3,2048]{1,0:T(4,128)S(1)} %copy-done.4), custom_call_target="tpu_custom_call" | custom-call | tf_op jit(solution)/shard_map/exchange_forces/pallas_call | solution.py:476
  45.6 0.6 %copy.12 = f32[3,2048]{1,0:T(4,128)} copy(f32[3,2048]{1,0:T(4,128)S(1)} %exchange_forces.1) | data formatting | bytes 49152
Async XLA Ops:
  0.7 0.8 %copy-start = (f32[3,2048]{1,0:T(4,128)S(1)}, f32[3,2048]{1,0:T(4,128)}, u32[]{:S(2)}) copy-start(f32[3,2048]{1,0:T(4,128)} %normal_ref.1) | copy-start | bytes 73732
  1.4 0.8 %copy-start.2 = (f32[3,2048]{1,0:T(4,128)S(1)}, f32[3,2048]{1,0:T(4,128)}, u32[]{:S(2)}) copy-start(f32[3,2048]{1,0:T(4,128)} %pos_hbm.1) | copy-start | bytes 73732
  2.2 0.8 %copy-start.3 = (f32[3,2048]{1,0:T(4,128)S(1)}, f32[3,2048]{1,0:T(4,128)}, u32[]{:S(2)}) copy-start(f32[3,2048]{1,0:T(4,128)} %centre_hbm.1) | copy-start | bytes 73732
  2.9 0.7 %copy-start.5 = (s32[1,2048]{1,0:T(1,128)S(1)}, s32[1,2048]{1,0:T(1,128)}, u32[]{:S(2)}) copy-start(s32[1,2048]{1,0:T(1,128)} %order_ref.1) | copy-start | bytes 24580
  3.6 28.6 %copy-start.1 = (f32[3,2048]{1,0:T(4,128)S(1)}, f32[3,2048]{1,0:T(4,128)}, u32[]{:S(2)}) copy-start(f32[3,2048]{1,0:T(4,128)} %normal_ref.1) | copy-start | bytes 73732
  3.6 28.6 %copy-start.4 = (s32[3,2048]{1,0:T(4,128)S(1)}, s32[3,2048]{1,0:T(4,128)}, u32[]{:S(2)}) copy-start(s32[3,2048]{1,0:T(4,128)} %corner_ref.1) | copy-start | bytes 73732
  3.6 28.6 %copy-start.6 = (s32[1,2048]{1,0:T(1,128)S(1)}, s32[1,2048]{1,0:T(1,128)}, u32[]{:S(2)}) copy-start(s32[1,2048]{1,0:T(1,128)} %order_ref.1) | copy-start | bytes 24580
  14.1 0.7 %copy-start.7 = (s32[1,1,128]{2,1,0:T(1,128)S(1)}, s32[1,1,128]{2,1,0:T(1,128)}, u32[]{:S(2)}) copy-start(s32[1,1,128]{2,1,0:T(1,128)} %param.14) | copy-start | bytes 1540
  14.8 0.7 %copy-start.8 = (s32[1,1,128,1]{2,3,1,0:T(1,128)S(1)}, s32[1,1,128,1]{2,3,1,0:T(1,128)}, u32[]{:S(2)}) copy-start(s32[1,1,128,1]{2,3,1,0:T(1,128)} %param.15) | copy-start | bytes 1540
  15.4 0.7 %copy-start.9 = (s32[1,1,128]{2,1,0:T(1,128)S(1)}, s32[1,1,128]{2,1,0:T(1,128)}, u32[]{:S(2)}) copy-start(s32[1,1,128]{2,1,0:T(1,128)} %param.16) | copy-start | bytes 1540

commit v4 on v2

--- a/solution.py
+++ b/solution.py
@@ -37,14 +37,14 @@
     return first, second, rest - second
 
 
-def facet_tables(centre_ref, normal_ref, geom_ref, wide_ref):
+def facet_tables(table_ref, geom_ref, wide_ref):
     scale = LOG2E / RADIUS_SQ
     nothing = jnp.zeros((1, BUCKET), F32)
 
     def prepare(b, carry):
         at = pl.ds(pl.multiple_of(b * BUCKET, BUCKET), BUCKET)
-        n = [normal_ref[k : k + 1, at] for k in range(3)]
-        c = [centre_ref[k : k + 1, at] for k in range(3)]
+        n = [table_ref[6 + k : 7 + k, at] for k in range(3)]
+        c = [table_ref[3 + k : 4 + k, at] for k in range(3)]
         n_c = n[0] * c[0] + n[1] * c[1] + n[2] * c[2]
         c_c = c[0] * c[0] + c[1] * c[1] + c[2] * c[2]
         gap = jnp.concatenate([-n[0], -n[1], -n[2], nothing, n_c] + [nothing] * 3, 0)
@@ -69,10 +69,8 @@
 
 def gather_kernel(
     domains,
-    pos_ref,
+    table_ref,
     order_ref,
-    centre_ref,
-    normal_ref,
     out_ref,
     geom_ref,
     wide_ref,
@@ -100,7 +98,7 @@
         picked = jnp.zeros((buckets, BUCKET), F32)
         for h in range(buckets):
             row = jnp.broadcast_to(
-                pos_ref[k : k + 1, h * BUCKET : (h + 1) * BUCKET], (buckets, BUCKET)
+                table_ref[k : k + 1, h * BUCKET : (h + 1) * BUCKET], (buckets, BUCKET)
             )
             found = jnp.take_along_axis(row, low, axis=1, mode="promise_in_bounds")
             picked = jnp.where(high == h, found, picked)
@@ -133,7 +131,7 @@
         )
 
     repeat(domains - 1, lambda t: copy_to(t).start())
-    facet_tables(centre_ref, normal_ref, geom_ref, wide_ref)
+    facet_tables(table_ref, geom_ref, wide_ref)
     repeat(domains - 1, lambda t: copy_from(t).wait_recv())
     repeat(domains - 1, lambda t: copy_to(t).wait_send())
 
@@ -141,9 +139,7 @@
 def pair_kernel(
     node_buckets,
     count_ref,
-    bucket_ref,
-    owner_ref,
-    slot_ref,
+    pair_ref,
     points_ref,
     geom_ref,
     wide_ref,
@@ -156,7 +152,7 @@
     odd_part,
 ):
     facet_buckets = geom_ref.shape[0]
-    slots = bucket_ref.shape[0]
+    slots = pair_ref.shape[0]
     for ref in (nodes_ref, odd_ref, even_sum, odd_sum):
         ref[...] = jnp.zeros_like(ref)
 
@@ -167,7 +163,12 @@
     spare = nodes_ref.shape[0] - 3 * node_buckets
 
     def base_of(p):
-        return owner_ref[p] * (3 * node_buckets) + slot_ref[p]
+        bucket = lax.div(pair_ref[p], facet_buckets)
+        owner = lax.div(bucket, node_buckets)
+        return owner * (3 * node_buckets) + (bucket - owner * node_buckets)
+
+    def facets_of(p):
+        return lax.rem(pair_ref[p], facet_buckets)
 
     def products(p, part_ref):
         base = base_of(p)
@@ -182,12 +183,12 @@
         value = jnp.where(place == 0, x, value)
         v1, v2, v3 = split3(value)
         table = jnp.concatenate([v1, v1, v1, v2, v2, v3, blank], 0).astype(BF16)
-        part_ref[...] = jnp.dot(geom_ref[bucket_ref[p]], table, preferred_element_type=F32)
+        part_ref[...] = jnp.dot(geom_ref[facets_of(p)], table, preferred_element_type=F32)
 
     def forces(p, part_ref, force_ref, sum_ref):
         live = p < count
         at = jnp.minimum(p, slots - 1)
-        b = bucket_ref[at]
+        b = facets_of(at)
         minus_gap, fade = part_ref[:BUCKET], part_ref[BUCKET:]
         small = jnp.exp(-jnp.abs(minus_gap))
         logs = jnp.where(small < 2.0**-8, small * (1.0 - 0.5 * small), jnp.log(1.0 + small))
@@ -347,6 +348,9 @@
     dma = pltpu.SemaphoreType.DMA
     shape = jax.ShapeDtypeStruct
 
+    packed = pair_owner.reshape(-1) * node_buckets + pair_slot.reshape(-1)
+    packed = packed * facet_buckets + pair_bucket.reshape(-1)
+
     points, geom, wide = pl.pallas_call(
         functools.partial(gather_kernel, domains),
         name="gather_points",
@@ -355,13 +359,13 @@
             shape((facet_buckets, 2 * BUCKET, BUCKET), BF16),
             shape((facet_buckets, 3, BUCKET, BUCKET), F32),
         ],
-        in_specs=[VMEM] * 4,
+        in_specs=[VMEM] * 2,
         out_specs=[VMEM] * 3,
         scratch_shapes=[dma((domains - 1,)), dma((domains - 1,))],
         compiler_params=pltpu.CompilerParams(
             collective_id=0, has_side_effects=True, vmem_limit_bytes=16 << 20
         ),
-    )(node_pos, node_order, facet_centroid, facet_normal)
+    )(jnp.concatenate([node_pos, facet_centroid, facet_normal], 0), node_order)
 
     nodes, rows = pl.pallas_call(
         functools.partial(pair_kernel, node_buckets),
@@ -370,7 +374,7 @@
             shape(((domains + 1) * size, BUCKET), F32),
             shape((facet_buckets, BUCKET), F32),
         ],
-        in_specs=[SMEM] * 4 + [VMEM] * 3,
+        in_specs=[SMEM] * 2 + [VMEM] * 3,
         out_specs=[VMEM] * 2,
         scratch_shapes=[
             pltpu.VMEM(((domains + 1) * size, BUCKET), F32),
@@ -382,9 +386,7 @@
         compiler_params=pltpu.CompilerParams(vmem_limit_bytes=32 << 20),
     )(
         pair_count,
-        pair_bucket.reshape(-1),
-        pair_owner.reshape(-1),
-        pair_slot.reshape(-1),
+        packed,
         points,
         geom,
         wide,

time: 44.2 us -> 41.7 us (0.943)
  local copies, waits for them, and re-layouts: 5.55 us -> 1.32 us
  other arithmetic: 0 us -> 1.52 us
  Pallas kernels: 37.4 us -> 37.9 us
    pallas_call x1, Pallas kernels: 12.8 us -> 20.1 us  [per_device(): pl.pallas_call(functools.partial(exchange_kernel, domains, copies), name=...]
    pallas_call x1, Pallas kernels: 15.1 us -> 8.26 us  [per_device(): pl.pallas_call(functools.partial(pair_kernel, node_buckets), name='pair_f...]
    unnamed x21 -> x9, local copies, waits for them, and re-layouts: 5.55 us -> 1.32 us
    concatenate x0 -> x1, other arithmetic: none -> 0.82 us  [per_device(): jnp.concatenate([node_pos, facet_centroid, facet_normal], 0)]
    add x0 -> x1, other arithmetic: none -> 0.69 us  [per_device(): packed = packed * facet_buckets + pair_bucket.reshape(-1)]
where the time goes in v4:
time: 41.7 us; the launch traced here: 41.4 us
  Pallas kernels  37.9 us (91%)
  other arithmetic  1.52 us (4%)
  local copies, waits for them, and re-layouts  1.32 us (3%)
  between operations  0.72 us (2%)
    pallas_call x1, Pallas kernels, per_device(): pl.pallas_call(functools.partial(exchange_kernel, domains, copies), name=...  20.1 us
    pallas_call x1, Pallas kernels, per_device(): pl.pallas_call(functools.partial(gather_kernel, domains), name='gather_po...  9.56 us
    pallas_call x1, Pallas kernels, per_device(): pl.pallas_call(functools.partial(pair_kernel, node_buckets), name='pair_f...  8.26 us
    unnamed x9, local copies, waits for them, and re-layouts  1.32 us

profile of v4, /device:TPU:0, one launch (start us, length us, event | category | flops | bytes accessed | tf_op | source)
XLA Modules:
  0.0 41.4 jit_solution(9157265702685793699)
XLA Ops:
  0.0 0.0 copy-start
  0.0 0.0 copy-start.3
  0.0 0.0 copy-start.1
  0.7 0.7 %bitcast_add_fusion.pair_ref = s32[128]{0:T(128)S(1)} fusion(s32[1,1,128]{2,1,0:T(1,128)} %param.14, s32[1,1,128]{2,1,0:T(1,128)} %param.16, s32[1,1,128,1]{2,3,1,0:T(1,128)} %param.15), kind=kLoop, calls=%fused_computation.1 | loop fusion | flops 512 | bytes 2048 | tf_op jit(solution)/shard_map/add | solution.py:352
  1.4 0.8 %pad_maximum_fusion.table_ref = f32[9,2048]{1,0:T(8,128)S(1)} fusion(f32[3,2048]{1,0:T(4,128)} %normal_ref.1, f32[3,2048]{1,0:T(4,128)} %param.11, f32[3,2048]{1,0:T(4,128)} %param.9), kind=kLoop, calls=%fused_computation | loop fusion | flops 36864 | bytes 147456 | tf_op jit(solution)/shard_map/concatenate | solution.py:368
  2.2 0.0 copy-start.2
  2.2 0.7 %copy-done.2 = s32[1,2048]{1,0:T(1,128)S(1)} copy-done((s32[1,2048]{1,0:T(1,128)S(1)}, s32[1,2048]{1,0:T(1,128)}, u32[]{:S(2)}) %copy-start.2) | copy-done | bytes 8216
  2.9 9.6 %gather_points.1 = (f32[384,128]{1,0:T(8,128)S(1)}, bf16[16,256,128]{2,1,0:T(8,128)(2,1)S(1)}, f32[16,3,128,128]{3,2,1,0:T(8,128)S(1)}) custom-call(f32[9,2048]{1,0:T(8,128)S(1)} %pad_maximum_fusion.table_ref, s32[1,2048]{1,0:T(1,128)S(1)} %copy-done.2), custom_call_target="tpu_custom_call" | custom-call | tf_op jit(solution)/shard_map/gather_points/pallas_call | solution.py:354
  12.5 8.3 %pair_forces.1 = (f32[432,128]{1,0:T(8,128)S(1)}, f32[16,128]{1,0:T(8,128)S(1)}) custom-call(s32[1,1]{1,0:T(1,128)S(6)} %copy.11.count_ref, s32[128]{0:T(128)S(1)} %bitcast_add_fusion.pair_ref, f32[384,128]{1,0:T(8,128)S(1)} %get-tuple-element.10.points_ref, bf16[16,256,128]{2,1,0:T(8,128)(2,1)S(1)} %get-tuple-element.11.geom_ref, ...), custom_call_target="tpu_custom_call" | custom-call | tf_op jit(solution)/shard_map/pair_forces/pallas_call | solution.py:370
  20.7 0.0 copy-done
  20.7 0.0 copy-done.3
  20.7 0.0 copy-done.1
  20.7 20.1 %exchange_forces.1 = f32[3,2048]{1,0:T(4,128)S(1)} custom-call(f32[432,128]{1,0:T(8,128)S(1)} %get-tuple-element.13.nodes_ref, f32[16,128]{1,0:T(8,128)S(1)} %get-tuple-element.14.rows_ref, f32[3,2048]{1,0:T(4,128)S(1)} %copy-done, s32[1,2048]{1,0:T(1,128)S(1)} %copy-done.3, s32[3,2048]{1,0:T(4,128)S(1)} %copy-done.1), custom_call_target="tpu_custom_call" | custom-call | tf_op jit(solution)/shard_map/exchange_forces/pallas_call | solution.py:395
  40.8 0.6 %copy.12 = f32[3,2048]{1,0:T(4,128)} copy(f32[3,2048]{1,0:T(4,128)S(1)} %exchange_forces.1) | data formatting | bytes 49152
Async XLA Ops:
  0.0 20.7 %copy-start = (f32[3,2048]{1,0:T(4,128)S(1)}, f32[3,2048]{1,0:T(4,128)}, u32[]{:S(2)}) copy-start(f32[3,2048]{1,0:T(4,128)} %normal_ref.1) | copy-start | bytes 73732
  0.0 20.7 %copy-start.3 = (s32[1,2048]{1,0:T(1,128)S(1)}, s32[1,2048]{1,0:T(1,128)}, u32[]{:S(2)}) copy-start(s32[1,2048]{1,0:T(1,128)} %order_ref.3) | copy-start | bytes 24580
  0.0 20.7 %copy-start.1 = (s32[3,2048]{1,0:T(4,128)S(1)}, s32[3,2048]{1,0:T(4,128)}, u32[]{:S(2)}) copy-start(s32[3,2048]{1,0:T(4,128)} %corner_ref.1) | copy-start | bytes 73732
  2.2 0.7 %copy-start.2 = (s32[1,2048]{1,0:T(1,128)S(1)}, s32[1,2048]{1,0:T(1,128)}, u32[]{:S(2)}) copy-start(s32[1,2048]{1,0:T(1,128)} %order_ref.3) | copy-start | bytes 24580
